TPU v7x, 256 devices: a whole 4x4x8 slice. The times are simulated.
256 devices in a mesh: replica: 16 (over z, core), seq: 4 (over x), tensor: 4 (over y).
Axes of the slice: x: 4, y: 4, z: 8, core: 2. Of those that a mesh axis runs over, the one named last changes fastest.
Arguments:
- residual: bfloat16 [16, 1024, 4096], P('replica'), may hold values from -15 to 15
- queries: bfloat16 [16, 1024, 4096], P('replica', 'seq', 'tensor'), may hold values from -40 to 40
- attn_keys: bfloat16 [16, 1024, 1024], P('replica', 'seq', 'tensor'), may hold values from -4 to 4
- attn_values: bfloat16 [16, 1024, 1024], P('replica', 'seq', 'tensor'), may hold values from -6 to 6
- lengths: int32 [16, 4], P('replica'), may hold values from 1 to 640, 1024 in all within a row
- requests: int32 [16, 4], P('replica'), may hold values from 1 to 256
- routes: int32 [16, 1024, 2], P('replica'), may hold values from 0 to 7, as said below
- out_weight: bfloat16 [4096, 4096], P('tensor', 'seq'), may hold values from -0.125 to 0.125
- norm_gain: float32 [4096], replicated, may hold values from 0.5 to 2
- router: bfloat16 [4096, 8], replicated, may hold values from -0.0234375 to 0.0234375
- w_gate: bfloat16 [1, 7168, 4096], P(None, ('seq', 'tensor')), may hold values from -0.09375 to 0.09375
- w_up: bfloat16 [1, 7168, 4096], P(None, ('seq', 'tensor')), may hold values from -0.09375 to 0.09375
- w_down: bfloat16 [1, 7168, 4096], P(None, ('seq', 'tensor')), may hold values from -0.09375 to 0.09375
Outputs:
- layer_out: bfloat16 [16, 1024, 4096], P('replica', 'seq', 'tensor')
Inputs may be any that keep to these rules, and one draw needn't show every extreme that they name: Each replica's lengths sum to 1024. `routes`: the two experts of a slot differ.
All inputs are finite; a program needn't handle non-finite values.
Results may differ from a plain program's by a relative error of at most 0.01.
Values may be sent and summed in bfloat16 or wider, within the bound.
A program may use at most 128 MiB of HBM per device.

v0:
```python
import functools
import math

import jax
import jax.numpy as jnp
from jax import lax
from jax.experimental import pallas as pl
from jax.experimental.pallas import tpu as pltpu
from jax.sharding import PartitionSpec as P

HEAD_DIM = 128
RING = 4
MESH = pl.DeviceIdType.MESH
VMEM = pltpu.VMEM
SIZES = (384, 640, 1024)

masked_score = -1e30
epsilon = 1e-05
f32 = jnp.float32
bf16 = jnp.bfloat16


class Copies:
    def __init__(self, send, recv):
        self.send, self.recv, self.count = send, recv, 0
        self.made = []

    def start(self, src, dst, where):
        n = self.count
        self.count += 1
        copy = pltpu.make_async_remote_copy(
            src_ref=src,
            dst_ref=dst,
            send_sem=self.send.at[n],
            recv_sem=self.recv.at[n],
            device_id=where,
            device_id_type=MESH,
        )
        copy.start()
        self.made.append(copy)
        return copy

    def drain(self):
        for copy in self.made:
            copy.wait_send()


class Ring:
    def __init__(self, axis):
        self.axis = axis
        self.me = lax.axis_index(axis)
        self.next = {axis: self.at(1)}
        self.prev = {axis: self.at(RING - 1)}

    def at(self, step):
        return lax.rem(self.me + step, RING)


def greet(devices):
    barrier = pltpu.get_barrier_semaphore()
    for device in devices:
        pl.semaphore_signal(barrier, inc=1, device_id=device, device_id_type=MESH)
    pl.semaphore_wait(barrier, len(devices))


def span(index, size):
    return pl.ds(pl.multiple_of(index * size, size), size)


class RingSum:
    def __init__(self, copies, ring, block, slots):
        self.copies, self.ring, self.block, self.slots = copies, ring, block, slots

    def raw(self):
        c, r, s = self.copies, self.ring, self.slots
        self.a = c.start(self.block(r.at(2), 0), s.at[0], r.next)
        self.b = c.start(self.block(r.at(2), 1), s.at[1], r.prev)
        self.c = c.start(self.block(r.at(1), 1), s.at[2], r.next)
        self.d = c.start(self.block(r.at(3), 0), s.at[3], r.prev)

    def middle(self):
        c, r, s = self.copies, self.ring, self.slots
        self.a.wait_recv()
        s[6] = (self.block(r.at(1), 0)[...].astype(f32) + s[0].astype(f32)).astype(bf16)
        self.e = c.start(s.at[6], s.at[4], r.next)
        self.b.wait_recv()
        s[7] = (self.block(r.at(3), 1)[...].astype(f32) + s[1].astype(f32)).astype(bf16)
        self.f = c.start(s.at[7], s.at[5], r.prev)

    def total(self, half):
        s = self.slots
        if half == 0:
            self.d.wait_recv()
            self.e.wait_recv()
            near, far = s[3], s[4]
        else:
            self.c.wait_recv()
            self.f.wait_recv()
            near, far = s[2], s[5]
        own = self.block(self.ring.me, half)[...]
        return own.astype(f32) + near.astype(f32) + far.astype(f32)


def attention_kernel(
    replicas, req_ref, len_ref, q_ref, k_ref, v_ref,
    att_ref, col_ref, lane_ref, most_ref,
    every, kv, bias, send, recv, req_send, req_recv,
):
    seq = Ring("seq")
    me = lax.axis_index("replica")
    rows = q_ref.shape[0]
    slots = RING * rows
    wide = k_ref.shape[1]
    kv_count = wide // HEAD_DIM
    group = q_ref.shape[1] // wide
    others = [{"replica": lax.rem(me + d, replicas)} for d in range(1, replicas)]
    greet([seq.next, seq.prev] + others)
    asked = Copies(req_send, req_recv)
    for other in others:
        asked.start(req_ref, every.at[me], other)
    c = Copies(send, recv)
    own_k, own_v = kv.at[seq.me, :, pl.ds(0, wide)], kv.at[seq.me, :, pl.ds(wide, wide)]
    first = [
        c.start(ref, place, where)
        for where in (seq.next, seq.prev)
        for ref, place in ((k_ref, own_k), (v_ref, own_v))
    ]
    kv[seq.me, :, pl.ds(0, wide)] = k_ref[...]
    kv[seq.me, :, pl.ds(wide, wide)] = v_ref[...]
    every[me] = req_ref[...]

    for copy in asked.made:
        copy.wait_recv()
    wanted = jnp.max(every[...], axis=1)
    lane = lax.broadcasted_iota(jnp.int32, wanted.shape, 1)
    admitted = jnp.where(lane == 0, wanted, 0.0)
    for b in range(1, RING):
        total = jnp.sum(
            jnp.sum(jnp.where(lane == b - 1, admitted, 0.0), axis=1, keepdims=True), axis=0, keepdims=True
        )
        scaled = wanted * float(replicas * rows // 4)
        share = jnp.floor(scaled / total)
        left = scaled - share * total
        share = jnp.where(left < 0, share - 1, jnp.where(left >= total, share + 1, share))
        admitted = jnp.where(lane == b, jnp.minimum(wanted, jnp.maximum(1.0, share)), admitted)
    most = jnp.max(jnp.sum(admitted, axis=1, keepdims=True), axis=0, keepdims=True)
    most_ref[...] = jnp.broadcast_to(most, most_ref.shape).astype(jnp.int32)
    mine = lax.broadcasted_iota(jnp.int32, wanted.shape, 0) == me
    row = jnp.sum(jnp.where(mine, admitted, 0.0), axis=0, keepdims=True)
    lane_one = lax.broadcasted_iota(jnp.int32, row.shape, 1)
    caps = [jnp.sum(jnp.where(lane_one == b, row, 0.0), axis=1, keepdims=True).astype(jnp.int32) for b in range(RING)]
    length = jnp.max(len_ref[...], axis=0, keepdims=True)
    lens = [jnp.sum(jnp.where(lane_one == b, length, 0.0), axis=1, keepdims=True).astype(jnp.int32) for b in range(RING)]

    def slot_of(place):
        found = jnp.full(place.shape, -1, jnp.int32)
        start = jnp.zeros((1, 1), jnp.int32)
        for b in range(RING):
            stop = start + caps[b]
            found = jnp.where((place >= start) & (place < stop), place - start + b * rows, found)
            start = stop
        return found

    col_ref[...] = slot_of(lax.broadcasted_iota(jnp.int32, col_ref.shape, 0))
    lane_ref[...] = slot_of(lax.broadcasted_iota(jnp.int32, lane_ref.shape, 1))

    key = lax.broadcasted_iota(jnp.int32, (1, slots), 1)
    live = jnp.zeros((1, slots), jnp.int32)
    for b in range(RING):
        live = jnp.where((key >= b * rows) & (key < b * rows + caps[b]), 1, live)
    query = lax.broadcasted_iota(jnp.int32, (rows, 1), 0) + seq.me * rows
    begin = jnp.zeros((rows, 1), jnp.int32)
    end = jnp.zeros((1, 1), jnp.int32)
    for j in range(RING):
        end = end + lens[j]
        begin = begin + jnp.where(end <= query, lens[j], 0)
    allowed = (key <= query) & (key >= begin) & ((live == 1) | (key == query))
    bias[...] = jnp.where(allowed, 0.0, masked_score)

    half = rows // 2
    first[0].wait_recv()
    first[1].wait_recv()
    before, after = kv.at[seq.at(3), pl.ds(0, half)], kv.at[seq.at(1), pl.ds(half, half)]
    on = c.start(before, before, seq.next)
    first[2].wait_recv()
    first[3].wait_recv()
    back = c.start(after, after, seq.prev)
    on.wait_recv()
    back.wait_recv()

    scale = 1.0 / math.sqrt(HEAD_DIM)
    span_g = group * HEAD_DIM
    sent = []
    for g in range(kv_count):
        keys = kv[:, :, g * HEAD_DIM:(g + 1) * HEAD_DIM].reshape(slots, HEAD_DIM)
        values = kv[:, :, wide + g * HEAD_DIM:wide + (g + 1) * HEAD_DIM].reshape(slots, HEAD_DIM)

        @pl.loop(0, group)
        def _(h):
            cols = span(h + g * group, HEAD_DIM)
            scores = lax.dot_general(
                q_ref[:, cols], keys, (((1,), (1,)), ((), ())), preferred_element_type=f32
            ) * scale + bias[...]
            highest = jnp.max(scores, axis=1, keepdims=True)
            weights = jnp.exp(scores - highest).astype(bf16)
            norm = jnp.sum(weights.astype(f32), axis=1, keepdims=True)
            out = jnp.dot(weights, values, preferred_element_type=f32)
            att_ref[span(seq.me, rows), cols] = (out / norm).astype(bf16)

        mine = att_ref.at[span(seq.me, rows), pl.ds(g * span_g, span_g)]
        sent.append((c.start(mine, mine, seq.next), c.start(mine, mine, seq.prev)))
    passed = []
    part = span_g // 2
    for g in range(kv_count):
        sent[g][0].wait_recv()
        there = att_ref.at[span(seq.at(3), rows), pl.ds(g * span_g, part)]
        passed.append(c.start(there, there, seq.next))
        sent[g][1].wait_recv()
        there = att_ref.at[span(seq.at(1), rows), pl.ds(g * span_g + part, part)]
        passed.append(c.start(there, there, seq.prev))
    for copy in passed:
        copy.wait_recv()
    asked.drain()
    c.drain()


def attend(replicas, requests, lengths, queries, keys, values):
    rows, cols = queries.shape
    slots = RING * rows
    groups = keys.shape[1] // HEAD_DIM
    count = 4 + 2 + 4 * groups
    vmem = pl.BlockSpec(memory_space=VMEM)
    return pl.pallas_call(
        functools.partial(attention_kernel, replicas),
        out_shape=(
            jax.ShapeDtypeStruct((slots, cols), bf16),
            jax.ShapeDtypeStruct((slots, 128), jnp.int32),
            jax.ShapeDtypeStruct((8, slots), jnp.int32),
            jax.ShapeDtypeStruct((8, 128), jnp.int32),
        ),
        in_specs=[vmem] * 5,
        out_specs=(vmem,) * 4,
        scratch_shapes=[
            VMEM((replicas, 8, 128), f32),
            VMEM((RING, rows, 2 * keys.shape[1]), bf16),
            VMEM((rows, slots), f32),
            pltpu.SemaphoreType.DMA((count,)),
            pltpu.SemaphoreType.DMA((count,)),
            pltpu.SemaphoreType.DMA((replicas - 1,)),
            pltpu.SemaphoreType.DMA((replicas - 1,)),
        ],
        compiler_params=pltpu.CompilerParams(
            collective_id=0, has_side_effects=True, vmem_limit_bytes=40 << 20
        ),
        name="attend",
    )(requests, lengths, queries, keys, values)


def stream_kernel(part_ref, res_ref, out_ref, slots, send, recv):
    seq, ten = Ring("seq"), Ring("tensor")
    rows, cols = res_ref.shape
    half, quarter = cols // 2, cols // 4
    greet([seq.next, seq.prev, ten.next, ten.prev])
    c = Copies(send, recv)
    summed = RingSum(
        c, ten, lambda b, h: part_ref.at[span(b, rows), pl.ds(h * half, half)], slots
    )
    summed.raw()
    summed.middle()

    def tile(t, s, h, q=None):
        if q is None:
            return out_ref.at[span(t, rows), pl.ds(pl.multiple_of(s * cols + h * half, half), half)]
        return out_ref.at[
            span(t, rows), pl.ds(pl.multiple_of(s * cols + h * half + q * quarter, quarter), quarter)
        ]

    def both(ref, ring):
        return c.start(ref, ref, ring.next), c.start(ref, ref, ring.prev)

    def hop(ref, where):
        return c.start(ref, ref, where)

    def place(h, first, second):
        return (first, second) if h == 1 else (second, first)

    near, wide_sends = {}, {}
    for h, ring in ((0, seq), (1, ten)):
        tile(ten.me, seq.me, h)[...] = (
            res_ref[:, h * half:(h + 1) * half].astype(f32) + summed.total(h)
        ).astype(bf16)
        near[h] = both(tile(ten.me, seq.me, h), ring)
    for h, other in ((0, ten), (1, seq)):
        wide_sends[h] = [both(tile(ten.me, seq.me, h), other)]

    def where_of(h, step):
        return (ten.me, seq.at(step)) if h == 0 else (ten.at(step), seq.me)

    far = {}
    for h, ring in ((0, seq), (1, ten)):
        near[h][0].wait_recv()
        t, s = where_of(h, 3)
        far[h] = [hop(tile(t, s, h, 0), ring.next)]
        near[h][1].wait_recv()
        t, s = where_of(h, 1)
        far[h].append(hop(tile(t, s, h, 1), ring.prev))
    for step in (3, 1):
        for h, other in ((0, ten), (1, seq)):
            t, s = where_of(h, step)
            wide_sends[h].append(both(tile(t, s, h), other))
    for h, other in ((0, ten), (1, seq)):
        far[h][0].wait_recv()
        far[h][1].wait_recv()
        t, s = where_of(h, 2)
        wide_sends[h].append(both(tile(t, s, h), other))
    last = []
    for i, step in enumerate((0, 3, 1, 2)):
        for h, other in ((0, ten), (1, seq)):
            t, s = where_of(h, step)

            def across(k):
                return (other.at(k), s) if h == 0 else (t, other.at(k))

            wide_sends[h][i][0].wait_recv()
            last.append(hop(tile(*across(3), h, 0), other.next))
            wide_sends[h][i][1].wait_recv()
            last.append(hop(tile(*across(1), h, 1), other.prev))
    for copy in last:
        copy.wait_recv()
    c.drain()


def gather_stream(partial_value, residual, collective_id):
    rows, cols = residual.shape
    vmem = pl.BlockSpec(memory_space=VMEM)
    count = 6 + 2 * (4 + 8 + 8)
    return pl.pallas_call(
        stream_kernel,
        out_shape=jax.ShapeDtypeStruct((RING * rows, RING * cols), bf16),
        in_specs=[vmem] * 2,
        out_specs=vmem,
        scratch_shapes=[
            VMEM((8, rows, cols // 2), bf16),
            pltpu.SemaphoreType.DMA((count,)),
            pltpu.SemaphoreType.DMA((count,)),
        ],
        compiler_params=pltpu.CompilerParams(
            collective_id=collective_id, has_side_effects=True, vmem_limit_bytes=40 << 20
        ),
        name="stream",
    )(partial_value, residual)


def mix_kernel(part_ref, own_ref, out_ref, slots, sums, late, send, recv):
    seq, ten = Ring("seq"), Ring("tensor")
    rows, cols = own_ref.shape
    half, quarter, eighth = cols // 2, cols // 4, cols // 8
    greet([seq.next, seq.prev, ten.next, ten.prev])
    c = Copies(send, recv)
    order = (2, 1, 3, 0)

    def term(row, col, h, q):
        return part_ref.at[
            span(row, rows), pl.ds(pl.multiple_of(col * cols + h * half + q * quarter, quarter), quarter)
        ]

    early = {0: [], 1: []}
    for i, step in enumerate(order):
        row, col = seq.at(step), ten.at(step)
        early[0].append(
            RingSum(c, ten, lambda b, q, row=row: term(row, b, 0, q), slots.at[0, i])
        )
        early[1].append(
            RingSum(c, seq, lambda b, q, col=col: term(b, col, 1, q), slots.at[1, i])
        )

    def raw(i):
        early[0][i].raw()
        early[1][i].raw()

    def middle(i):
        early[0][i].middle()
        early[1][i].middle()

    def finish(i):
        for h, ring in ((0, seq), (1, ten)):
            for q in range(2):
                sums[h, ring.at(order[i]), :, q * quarter:(q + 1) * quarter] = (
                    early[h][i].total(q).astype(bf16)
                )

    raw(0)
    raw(1)
    for i in range(RING):
        middle(i)
        if i + 2 < RING:
            raw(i + 2)
    for i in range(RING):
        finish(i)
    final = [
        RingSum(
            c,
            ring,
            lambda b, q, h=h: sums.at[h, b, :, pl.ds(q * quarter, quarter)],
            late.at[h],
        )
        for h, ring in ((0, seq), (1, ten))
    ]
    for f in final:
        f.raw()
    for f in final:
        f.middle()
    sent = []
    for h in range(2):
        for q in range(2):
            at = h * half + q * quarter
            mine = out_ref.at[span(seq.me, rows), pl.ds(at, quarter)]
            mine[...] = (
                own_ref[:, at:at + quarter].astype(f32) + final[h].total(q)
            ).astype(bf16)
            sent.append((c.start(mine, mine, seq.next), c.start(mine, mine, seq.prev)))
    passed = []
    for k in range(4):
        at = k * quarter
        sent[k][0].wait_recv()
        there = out_ref.at[span(seq.at(3), rows), pl.ds(at, eighth)]
        passed.append(c.start(there, there, seq.next))
        sent[k][1].wait_recv()
        there = out_ref.at[span(seq.at(1), rows), pl.ds(at + eighth, eighth)]
        passed.append(c.start(there, there, seq.prev))
    for copy in passed:
        copy.wait_recv()
    c.drain()


def gather_mixed(partial_out, own_stream, collective_id):
    rows, cols = own_stream.shape
    vmem = pl.BlockSpec(memory_space=VMEM)
    count = 10 * 6 + 16
    return pl.pallas_call(
        mix_kernel,
        out_shape=jax.ShapeDtypeStruct((RING * rows, cols), bf16),
        in_specs=[vmem] * 2,
        out_specs=vmem,
        scratch_shapes=[
            VMEM((2, RING, 8, rows, cols // 4), bf16),
            VMEM((2, RING, rows, cols // 2), bf16),
            VMEM((2, 8, rows, cols // 4), bf16),
            pltpu.SemaphoreType.DMA((count,)),
            pltpu.SemaphoreType.DMA((count,)),
        ],
        compiler_params=pltpu.CompilerParams(
            collective_id=collective_id, has_side_effects=True, vmem_limit_bytes=50 << 20
        ),
        name="mix",
    )(partial_out, own_stream)


def dot(a, b, contract):
    return lax.dot_general(a, b, (contract, ((), ())), preferred_element_type=f32)


def packed_layer(
    size, index, attended, slot_col, slot_lane, residual, routes, out_weight, norm_gain, router, w_gate, w_up, w_down
):
    slots = attended.shape[0]
    rows_dev = slots // RING
    piece = size // RING
    seq_index = lax.axis_index("seq")
    tensor_index = lax.axis_index("tensor")
    positions = jnp.arange(slots, dtype=jnp.int32)
    width = out_weight.shape[1]
    pick = (slot_col[:size] == positions[None, :]).astype(bf16)
    packed = dot(pick, attended, ((1,), (0,))).astype(bf16)
    partial_value = dot(packed, out_weight, ((1,), (0,))).astype(bf16)
    own_pick = lax.dynamic_slice(slot_col, (tensor_index * piece, 0), (piece, 1))
    own_res = dot(
        (own_pick == positions[None, :]).astype(bf16),
        lax.dynamic_slice(residual, (0, seq_index * width), (slots, width)),
        ((1,), (0,)),
    ).astype(bf16)
    stream = gather_stream(partial_value, own_res, 1 + 2 * index)
    wide = stream.astype(f32)
    normed = (
        wide * lax.rsqrt(jnp.mean(wide * wide, axis=1, keepdims=True) + epsilon) * norm_gain
    ).astype(bf16)
    chosen = dot(pick, routes.astype(bf16), ((1,), (0,))).astype(jnp.int32)
    logits = dot(normed, router, ((1,), (0,)))
    expert_ids = jnp.arange(router.shape[1], dtype=jnp.int32)
    first = jnp.sum(jnp.where(chosen[:, 0:1] == expert_ids[None, :], logits, 0.0), axis=1, keepdims=True)
    second = jnp.sum(jnp.where(chosen[:, 1:2] == expert_ids[None, :], logits, 0.0), axis=1, keepdims=True)
    weight_first = jax.nn.sigmoid(first - second)
    weight_second = jax.nn.sigmoid(second - first)
    partial_out = None
    for e in range(w_gate.shape[0]):
        combine = jnp.where(chosen[:, 0:1] == e, weight_first, 0.0) + jnp.where(
            chosen[:, 1:2] == e, weight_second, 0.0
        )
        gate = dot(normed, w_gate[e], ((1,), (1,)))
        upward = dot(normed, w_up[e], ((1,), (1,)))
        hidden = (jax.nn.silu(gate) * upward * combine).astype(bf16)
        down = dot(hidden, w_down[e], ((1,), (0,)))
        partial_out = down if partial_out is None else partial_out + down
    own_stream = lax.dynamic_slice(stream, (seq_index * piece, tensor_index * width), (piece, width))
    packed_out = gather_mixed(partial_out.astype(bf16), own_stream, 2 + 2 * index)
    query_pos = seq_index * rows_dev + jnp.arange(rows_dev, dtype=jnp.int32)
    spread = (query_pos[:, None] == slot_lane[:1, :size]).astype(bf16)
    return dot(spread, packed_out, ((1,), (0,))).astype(bf16)


def shards(
    residual, queries, attn_keys, attn_values, lengths, requests, routes,
    out_weight, norm_gain, router, w_gate, w_up, w_down,
):
    replicas = lax.axis_size("replica")

    def widened(row):
        return jnp.broadcast_to(jnp.pad(row.astype(f32), ((0, 0), (0, 128 - row.shape[1]))), (8, 128))

    attended, slot_col, slot_lane, most = attend(
        replicas, widened(requests), widened(lengths), queries[0], attn_keys[0], attn_values[0]
    )
    slots = attended.shape[0]
    sizes = [n for n in SIZES if n < slots] + [slots]
    choice = jnp.sum(most[0, 0] > jnp.array(sizes[:-1], jnp.int32)).astype(jnp.int32)
    out = lax.switch(
        choice,
        [functools.partial(packed_layer, n, i) for i, n in enumerate(sizes)],
        attended, slot_col[:, :1], slot_lane, residual[0], routes[0],
        out_weight, norm_gain, router, w_gate, w_up, w_down,
    )
    return out[None]


def solution(mesh):
    return jax.shard_map(
        shards,
        mesh=mesh,
        in_specs=(
            P("replica", None, None),
            P("replica", "seq", "tensor"),
            P("replica", "seq", "tensor"),
            P("replica", "seq", "tensor"),
            P("replica", None),
            P("replica", None),
            P("replica", None, None),
            P("tensor", "seq"),
            P(),
            P(),
            P(None, ("seq", "tensor"), None),
            P(None, ("seq", "tensor"), None),
            P(None, ("seq", "tensor"), None),
        ),
        out_specs=P("replica", "seq", "tensor"),
        check_vma=False,
    )
```

profile of v0, /device:TPU:32, one launch (start us, length us, event | category | flops | bytes accessed | tf_op | source)
XLA Modules:
  0.0 188.6 jit_solution(13637919056383818190)
XLA Ops:
  0.0 0.7 convert_element_type.111
  0.7 0.7 convert_element_type.112
  1.3 1.0 copy-done.4
  2.4 0.9 copy-done.5
  3.3 0.9 copy-done.6
  4.2 42.2 %attend.1 = (bf16[1024,1024]{1,0:T(8,128)(2,1)S(1)}, s32[1024,128]{1,0:T(8,128)S(1)}, s32[8,1024]{1,0:T(8,128)S(1)}, s32[8,128]{1,0:T(8,128)S(1)}) custom-call(f32[8,128]{1,0:T(8,128)S(1)} %broadcast_in_dim.82.req_ref, f32[8,128]{1,0:T(8,128)S(1)} %broadcast_in_dim.84.len_ref, bf16[256,1024]{1,0:T(8,128)(2,1)S(1)} %bitcast.87, ...), custom_call_target="tpu_custom_call" | custom-call | tf_op jit(solution)/shard_map/attend/pallas_call | solution.py:233
  46.4 0.5 slice.45
  46.9 2.0 %fusion.135 = s32[]{:T(128)} fusion(s32[2]{0:T(128)} %constant.97.clone, s32[]{:T(128)} %bitcast.27), kind=kLoop, calls=%fused_computation.158 | loop fusion | flops 5 | bytes 16 | tf_op jit(solution)/shard_map/reduce_sum | solution.py:525
  49.6 137.8 %conditional.1 = (bf16[1,256,1024]{2,1,0:T(8,128)(2,1)S(1)}) conditional(s32[]{:T(128)} %clamp.3, (s32[8,1024]{1,0:T(8,128)S(1)}, s32[1024,1]{1,0:T(8,128)S(1)}, bf16[1024,1024]{1,0:T(8,128)(2,1)S(1)}, bf16[1024,1024]{1,0:T(8,128)(2,1)}, bf16[1024,4096]{1,0:T(8,128)(2,1)}, /*index=5*/f32[4096]{0:T(1024)}, ...), branch_computations={%region_1.5_spmd, %region_5.9_spmd, %region_9.13_spmd} | conditional | flops 16789929984 | bytes 126453144 | solution.py:526
  58.3 0.0 copy-start.11
  58.3 1.3 copy-done.11
  59.6 0.2 copy.19
  59.8 0.1 constant_dynamic-slice_fusion.1
  59.9 2.2 %fusion.115.res_ref = bf16[160,1024]{1,0:T(8,128)(2,1)S(1)} fusion(bf16[1024,4096]{1,0:T(8,128)(2,1)} %get-tuple-element.91, s32[]{:T(128)S(6)} %select_n.63, s32[160]{0:T(256)S(1)} %bitcast.100), kind=kOutput, calls=%fused_computation.129 | convolution fusion | flops 335872000 | bytes 2425476 | tf_op jit(solution)/shard_map/cond/branch_1_fun/dot_general | solution.py:460
  62.1 5.1 %convolution_convert_fusion.6.part_ref = bf16[640,1024]{1,0:T(8,128)(2,1)S(1)} fusion(bf16[1024,1024]{1,0:T(8,128)(2,1)} %get-tuple-element.90, bf16[1024,1024]{1,0:T(8,128)(2,1)} %copy-done.11, s32[640]{0:T(1024)S(1)} %slice_reduce_fusion.4), kind=kOutput, calls=%fused_computation.121 | convolution fusion | flops 2686320640 | bytes 5507584 | tf_op jit(solution)/shard_map/cond/branch_1_fun/dot_general | solution.py:460
  67.2 42.0 %stream.4 = bf16[640,4096]{1,0:T(8,128)(2,1)S(1)} custom-call(bf16[640,1024]{1,0:T(8,128)(2,1)S(1)} %convolution_convert_fusion.6.part_ref, bf16[160,1024]{1,0:T(8,128)(2,1)S(1)} %fusion.115.res_ref), custom_call_target="tpu_custom_call" | custom-call | tf_op jit(solution)/shard_map/cond/branch_1_fun/stream/pallas_call | solution.py:337
  109.3 0.0 copy-start.1
  109.3 0.0 copy-start.20
  109.3 0.0 copy-start.14
  109.3 0.0 copy-start.17
  109.3 1.1 fusion.90
  110.4 0.6 fusion.118
  111.1 0.0 copy-start.9
  111.1 1.5 select_reduce_fusion.5
  112.7 0.4 copy-done.9
  113.1 3.1 %fusion.96 = f32[640,448]{0,1:T(8,128)S(1)} fusion(bf16[1,448,4096]{2,1,0:T(8,128)(2,1)S(1)} %copy-done.9, bf16[640,4096]{1,0:T(8,128)(2,1)S(1)} %stream.4, f32[4096]{0:T(1024)S(1)} %copy-done.17, f32[640]{0:T(1024)S(1)} %add_rsqrt_fusion.2), kind=kOutput, calls=%fused_computation.113 | convolution fusion | flops 2359296000 | bytes 10078720 | tf_op jit(solution)/shard_map/cond/branch_1_fun/dot_general | solution.py:460
  116.3 15.3 %convolution_convert_fusion.5.part_ref = bf16[640,4096]{1,0:T(8,128)(2,1)} fusion(bf16[1,448,4096]{2,1,0:T(8,128)(2,1)} %get-tuple-element.97, bf16[1,448,4096]{2,1,0:T(8,128)(2,1)} %get-tuple-element.94, f32[640,448]{0,1:T(8,128)S(1)} %fusion.96, f32[640]{0:T(1024)S(1)} %fusion.127, bf16[640,4096]{1,0:T(8,128)(2,1)} %copy-done.1, ...), kind=kOutput, calls=%fused_computation.109 | convolution fusion | flops 4712734720 | bytes 18994176 | tf_op jit(solution)/shard_map/cond/branch_1_fun/dot_general | solution.py:460
  131.5 1.0 dynamic_slice.23.own_ref
  132.5 46.1 %mix.4 = bf16[640,1024]{1,0:T(8,128)(2,1)S(1)} custom-call(bf16[640,4096]{1,0:T(8,128)(2,1)} %convolution_convert_fusion.5.part_ref, bf16[160,1024]{1,0:T(8,128)(2,1)S(1)} %dynamic_slice.23.own_ref), custom_call_target="tpu_custom_call" | custom-call | tf_op jit(solution)/shard_map/cond/branch_1_fun/mix/pallas_call | solution.py:440
  178.6 0.6 fusion.114
  187.5 0.0 copy-start.7
  187.5 0.8 copy-done.7
  (18 shorter events, 0.1 us)
Async XLA Ops:
  1.3 1.0 copy-start.4
  2.4 0.9 copy-start.5
  3.3 0.9 copy-start.6
  58.3 1.4 copy-start.11
  109.3 3.4 %copy-start.1 = (bf16[640,4096]{1,0:T(8,128)(2,1)}, bf16[640,4096]{1,0:T(8,128)(2,1)S(1)}, u32[]{:S(2)}) copy-start(bf16[640,4096]{1,0:T(8,128)(2,1)S(1)} %stream.4) | copy-start | bytes 15728644 | tf_op jit(solution)/shard_map/cond
  109.3 1.1 copy-start.20
  109.3 1.8 copy-start.14
  109.3 1.8 copy-start.17
  111.1 2.0 %copy-start.9 = (bf16[1,448,4096]{2,1,0:T(8,128)(2,1)S(1)}, bf16[1,448,4096]{2,1,0:T(8,128)(2,1)}, u32[]{:S(2)}) copy-start(bf16[1,448,4096]{2,1,0:T(8,128)(2,1)} %get-tuple-element.93) | copy-start | bytes 11010052 | tf_op jit(solution)/shard_map/cond
  187.5 0.8 copy-start.7
where the time goes:
time: 192 us; the launch traced here: 189 us
  Pallas kernels  130 us (68%)
  matrix products  28.4 us (15%)
  loops' own time  17 us (9%)
  local copies, waits for them, and re-layouts  7.26 us (4%)
  other arithmetic  4.46 us (2%)
    pallas_call x1, Pallas kernels, gather_mixed(): pl.pallas_call(mix_kernel, out_shape=jax.ShapeDtypeStruct((RING * rows, c...  46.1 us
    pallas_call x1, Pallas kernels, attend(): pl.pallas_call(functools.partial(attention_kernel, replicas), out_shape=(...  42.2 us
    pallas_call x1, Pallas kernels, gather_stream(): pl.pallas_call(stream_kernel, out_shape=jax.ShapeDtypeStruct((RING * rows...  42 us
    dot_general x7, matrix products, dot(): lax.dot_general(a, b, (contract, ((), ())), preferred_element_type=f32)  28.4 us
    another operation x1, loops' own time, shards(): lax.switch(choice, [functools.partial(packed_layer, n, i) for i, n in enu...  17 us

commit v1 on v0

v1 whole, which is shorter than its diff:
```python
import functools
import math

import jax
import jax.numpy as jnp
from jax import lax
from jax.experimental import pallas as pl
from jax.experimental.pallas import tpu as pltpu
from jax.sharding import PartitionSpec as P

HEAD_DIM = 128
RING = 4
MESH = pl.DeviceIdType.MESH
VMEM = pltpu.VMEM
WINDOW = 640

masked_score = -1e30
epsilon = 1e-05
f32 = jnp.float32
bf16 = jnp.bfloat16


class Copies:
    def __init__(self, send, recv):
        self.send, self.recv, self.count = send, recv, 0
        self.made = []

    def start(self, src, dst, where):
        n = self.count
        self.count += 1
        copy = pltpu.make_async_remote_copy(
            src_ref=src,
            dst_ref=dst,
            send_sem=self.send.at[n],
            recv_sem=self.recv.at[n],
            device_id=where,
            device_id_type=MESH,
        )
        copy.start()
        self.made.append(copy)
        return copy

    def drain(self):
        for copy in self.made:
            copy.wait_send()


class Ring:
    def __init__(self, axis):
        self.axis = axis
        self.me = lax.axis_index(axis)
        self.next = {axis: self.at(1)}
        self.prev = {axis: self.at(RING - 1)}

    def at(self, step):
        return lax.rem(self.me + step, RING)


def greet(devices):
    barrier = pltpu.get_barrier_semaphore()
    for device in devices:
        pl.semaphore_signal(barrier, inc=1, device_id=device, device_id_type=MESH)
    pl.semaphore_wait(barrier, len(devices))


def span(index, size):
    return pl.ds(pl.multiple_of(index * size, size), size)


def dot(a, b, contract):
    return lax.dot_general(a, b, (contract, ((), ())), preferred_element_type=f32)


PLAIN = ((1,), (0,))
TURNED = ((1,), (1,))


class RingSum:
    def __init__(self, copies, ring, block, slots):
        self.copies, self.ring, self.block, self.slots = copies, ring, block, slots

    def far(self):
        c, r, s = self.copies, self.ring, self.slots
        self.a = c.start(self.block(2, 0), s.at[0], r.next)
        self.b = c.start(self.block(2, 1), s.at[1], r.prev)

    def ahead(self):
        self.c = self.copies.start(self.block(1, 1), self.slots.at[2], self.ring.next)

    def behind(self):
        self.d = self.copies.start(self.block(3, 0), self.slots.at[3], self.ring.prev)

    def raw(self):
        self.far()
        self.ahead()
        self.behind()

    def middle(self):
        c, r, s = self.copies, self.ring, self.slots
        self.a.wait_recv()
        s[6] = (self.block(1, 0)[...].astype(f32) + s[0].astype(f32)).astype(bf16)
        self.e = c.start(s.at[6], s.at[4], r.next)
        self.b.wait_recv()
        s[7] = (self.block(3, 1)[...].astype(f32) + s[1].astype(f32)).astype(bf16)
        self.f = c.start(s.at[7], s.at[5], r.prev)

    def total(self, half):
        s = self.slots
        if half == 0:
            self.d.wait_recv()
            self.e.wait_recv()
            near, far = s[3], s[4]
        else:
            self.c.wait_recv()
            self.f.wait_recv()
            near, far = s[2], s[5]
        own = self.block(0, half)[...]
        return own.astype(f32) + near.astype(f32) + far.astype(f32)


def attention_kernel(
    replicas, req_ref, len_ref, routes_ref, q_hbm, k_hbm, v_hbm, w_hbm, res_hbm,
    part_ref, own_ref, delta_ref, lane_ref, most_ref,
    req, every, q_ref, kv, bias, pick, att_ref, w_ref, res_ref, proj,
    local, send, recv, req_send, req_recv,
):
    seq = Ring("seq")
    me = lax.axis_index("replica")
    rows = q_ref.shape[0]
    slots = RING * rows
    wide = k_hbm.shape[1]
    kv_count = wide // HEAD_DIM
    group = q_ref.shape[1] // wide
    cols = w_ref.shape[1]
    loads = [
        pltpu.make_async_copy(src, dst, local.at[i])
        for i, (src, dst) in enumerate((
            (k_hbm, kv.at[seq.me, :, pl.ds(0, wide)]),
            (v_hbm, kv.at[seq.me, :, pl.ds(wide, wide)]),
            (q_hbm, q_ref),
            (res_hbm.at[:, span(seq.me, cols)], res_ref),
            (w_hbm, w_ref),
        ))
    ]
    for load in loads:
        load.start()
    req[...] = jnp.zeros_like(req)
    req[0:1, 0:RING] = req_ref[...].astype(f32)
    others = [{"replica": lax.rem(me + d, replicas)} for d in range(1, replicas)]
    greet([seq.next, seq.prev] + others)
    c = Copies(send, recv)
    loads[0].wait()
    loads[1].wait()
    first = [c.start(kv.at[seq.me], kv.at[seq.me], where) for where in (seq.next, seq.prev)]
    asked = Copies(req_send, req_recv)
    for other in others:
        asked.start(req, every.at[me], other)
    every[me] = req[...]

    for copy in asked.made:
        copy.wait_recv()
    wanted = jnp.max(every[...], axis=1)
    lane = lax.broadcasted_iota(jnp.int32, wanted.shape, 1)
    admitted = jnp.where(lane == 0, wanted, 0.0)
    for b in range(1, RING):
        total = jnp.sum(
            jnp.sum(jnp.where(lane == b - 1, admitted, 0.0), axis=1, keepdims=True), axis=0, keepdims=True
        )
        scaled = wanted * float(replicas * rows // 4)
        share = jnp.floor(scaled / total)
        left = scaled - share * total
        share = jnp.where(left < 0, share - 1, jnp.where(left >= total, share + 1, share))
        admitted = jnp.where(lane == b, jnp.minimum(wanted, jnp.maximum(1.0, share)), admitted)
    most = jnp.max(jnp.sum(admitted, axis=1, keepdims=True), axis=0, keepdims=True)
    most_ref[...] = jnp.broadcast_to(most, most_ref.shape).astype(jnp.int32)
    mine = lax.broadcasted_iota(jnp.int32, wanted.shape, 0) == me
    row = jnp.sum(jnp.where(mine, admitted, 0.0), axis=0, keepdims=True)
    lane_one = lax.broadcasted_iota(jnp.int32, row.shape, 1)
    caps = [jnp.sum(jnp.where(lane_one == b, row, 0.0), axis=1, keepdims=True).astype(jnp.int32) for b in range(RING)]
    prompts = len_ref.shape[1]
    length = len_ref[...].astype(f32)
    lane_len = lax.broadcasted_iota(jnp.int32, length.shape, 1)
    lens = [
        jnp.sum(jnp.where(lane_len == b, length, 0.0), axis=1, keepdims=True).astype(jnp.int32)
        for b in range(prompts)
    ]

    def slot_of(place):
        found = jnp.full(place.shape, -1, jnp.int32)
        start = jnp.zeros((1, 1), jnp.int32)
        for b in range(RING):
            stop = start + caps[b]
            found = jnp.where((place >= start) & (place < stop), place - start + b * rows, found)
            start = stop
        return found

    lane_ref[...] = slot_of(lax.broadcasted_iota(jnp.int32, lane_ref.shape, 1))
    key = lax.broadcasted_iota(jnp.int32, (1, slots), 1)
    live = jnp.zeros((1, slots), jnp.int32)
    for b in range(RING):
        live = jnp.where((key >= b * rows) & (key < b * rows + caps[b]), 1, live)
    query = lax.broadcasted_iota(jnp.int32, (rows, 1), 0) + seq.me * rows
    begin = jnp.zeros((rows, 1), jnp.int32)
    end = jnp.zeros((1, 1), jnp.int32)
    for j in range(prompts):
        end = end + lens[j]
        begin = begin + jnp.where(end <= query, lens[j], 0)
    allowed = (key <= query) & (key >= begin) & ((live == 1) | (key == query))
    bias[...] = jnp.where(allowed, 0.0, masked_score)

    half = rows // 2
    first[0].wait_recv()
    before, after = kv.at[seq.at(3), pl.ds(0, half)], kv.at[seq.at(1), pl.ds(half, half)]
    on = c.start(before, before, seq.next)
    first[1].wait_recv()
    back = c.start(after, after, seq.prev)

    @pl.loop(0, slots // 128)
    def _(i):
        place = lax.broadcasted_iota(jnp.int32, (128, 1), 0) + i * 128
        pick[span(i, 128), :] = jnp.where(slot_of(place) == key, 1.0, 0.0).astype(bf16)

    expert = lax.broadcasted_iota(jnp.int32, (128, slots), 0)
    gap = jnp.where(routes_ref[0:1, :] == expert, 1.0, 0.0) - jnp.where(routes_ref[1:2, :] == expert, 1.0, 0.0)
    delta_ref[...] = dot(pick[...], gap.astype(bf16), TURNED)
    on.wait_recv()
    back.wait_recv()
    loads[2].wait()

    scale = 1.0 / math.sqrt(HEAD_DIM)
    span_g = group * HEAD_DIM
    sent = []
    for g in range(kv_count):
        keys = kv[:, :, g * HEAD_DIM:(g + 1) * HEAD_DIM].reshape(slots, HEAD_DIM)
        values = kv[:, :, wide + g * HEAD_DIM:wide + (g + 1) * HEAD_DIM].reshape(slots, HEAD_DIM)

        @pl.loop(0, group)
        def _(h):
            at = span(h + g * group, HEAD_DIM)
            scores = dot(q_ref[:, at], keys, TURNED) * scale + bias[...]
            highest = jnp.max(scores, axis=1, keepdims=True)
            weights = jnp.exp(scores - highest).astype(bf16)
            norm = jnp.sum(weights.astype(f32), axis=1, keepdims=True)
            att_ref[span(seq.me, rows), at] = (dot(weights, values, PLAIN) / norm).astype(bf16)

        mine = att_ref.at[span(seq.me, rows), pl.ds(g * span_g, span_g)]
        sent.append((c.start(mine, mine, seq.next), c.start(mine, mine, seq.prev)))

    def project(block, start):
        proj[...] = dot(att_ref[span(block, rows), :], w_ref[...], PLAIN).astype(bf16)

        @pl.loop(0, RING)
        def _(i):
            chosen = dot(pick[span(i, rows), span(block, rows)], proj[...], PLAIN)
            if not start:
                chosen = chosen + part_ref[span(i, rows), :].astype(f32)
            part_ref[span(i, rows), :] = chosen.astype(bf16)

    loads[3].wait()

    @pl.loop(0, RING)
    def _(i):
        own_ref[span(i, rows), :] = dot(pick[span(i, rows), :], res_ref[...], PLAIN).astype(bf16)

    loads[4].wait()
    project(seq.me, True)
    passed = []
    part = span_g // 2
    for g in range(kv_count):
        sent[g][0].wait_recv()
        there = att_ref.at[span(seq.at(3), rows), pl.ds(g * span_g, part)]
        passed.append(c.start(there, there, seq.next))
        sent[g][1].wait_recv()
        there = att_ref.at[span(seq.at(1), rows), pl.ds(g * span_g + part, part)]
        passed.append(c.start(there, there, seq.prev))
    project(seq.at(3), False)
    project(seq.at(1), False)
    for copy in passed:
        copy.wait_recv()
    project(seq.at(2), False)
    asked.drain()
    c.drain()


def attend(replicas, requests, lengths, routes, queries, keys, values, out_weight, residual):
    rows, heads = queries.shape
    slots = RING * rows
    cols = out_weight.shape[1]
    groups = keys.shape[1] // HEAD_DIM
    count = 4 + 4 * groups
    vmem = pl.BlockSpec(memory_space=VMEM)
    hbm = pl.BlockSpec(memory_space=pltpu.HBM)
    dma = pltpu.SemaphoreType.DMA
    return pl.pallas_call(
        functools.partial(attention_kernel, replicas),
        out_shape=(
            jax.ShapeDtypeStruct((slots, cols), bf16),
            jax.ShapeDtypeStruct((slots, cols), bf16),
            jax.ShapeDtypeStruct((slots, 128), f32),
            jax.ShapeDtypeStruct((8, slots), jnp.int32),
            jax.ShapeDtypeStruct((8, 128), jnp.int32),
        ),
        in_specs=[vmem] * 3 + [hbm] * 5,
        out_specs=(vmem,) * 5,
        scratch_shapes=[
            VMEM((8, 128), f32),
            VMEM((replicas, 8, 128), f32),
            VMEM((rows, heads), bf16),
            VMEM((RING, rows, 2 * keys.shape[1]), bf16),
            VMEM((rows, slots), f32),
            VMEM((slots, slots), bf16),
            VMEM((slots, heads), bf16),
            VMEM(out_weight.shape, bf16),
            VMEM((slots, cols), bf16),
            VMEM((rows, cols), bf16),
            dma((5,)), dma((count,)), dma((count,)), dma((replicas - 1,)), dma((replicas - 1,)),
        ],
        compiler_params=pltpu.CompilerParams(
            collective_id=0, has_side_effects=True, vmem_limit_bytes=58 << 20
        ),
        name="attend",
    )(requests, lengths, routes, queries, keys, values, out_weight, residual)


def layer_kernel(
    part_ref, res_ref, delta_ref, lane_ref, gain_ref, router_ref, gate_hbm, up_hbm, down_hbm,
    out_ref,
    stream, mixed, normed, hidden, combine, packed, w_gate, w_up, w_down,
    slots_c, slots_y, slots_x, sums_y, sums_x, late_y, late_x, local, send, recv,
):
    seq, ten = Ring("seq"), Ring("tensor")
    rows, cols = res_ref.shape
    features = stream.shape[1]
    half, quarter = cols // 2, cols // 4
    loads = [
        pltpu.make_async_copy(src, dst, local.at[i])
        for i, (src, dst) in enumerate(((gate_hbm, w_gate), (up_hbm, w_up), (down_hbm, w_down)))
    ]
    for load in loads:
        load.start()
    greet([seq.next, seq.prev, ten.next, ten.prev])
    c = Copies(send, recv)

    def both(ref, ring):
        return c.start(ref, ref, ring.next), c.start(ref, ref, ring.prev)

    def hop(ref, where):
        return c.start(ref, ref, where)

    summed = RingSum(
        c, ten, lambda k, h: part_ref.at[span(ten.at(k), rows), pl.ds(h * half, half)], slots_c
    )
    summed.raw()
    summed.middle()

    def tile(t, s, h, q=None):
        width, start = (half, h * half) if q is None else (quarter, h * half + q * quarter)
        return stream.at[span(t, rows), pl.ds(pl.multiple_of(s * cols + start, width), width)]

    def where_of(h, step):
        return (ten.me, seq.at(step)) if h == 0 else (ten.at(step), seq.me)

    firsts, seconds = ((0, seq), (1, ten)), ((0, ten), (1, seq))
    near, wide, far, last = {}, {}, {}, []
    for h, ring in firsts:
        tile(ten.me, seq.me, h)[...] = (
            res_ref[:, h * half:(h + 1) * half].astype(f32) + summed.total(h)
        ).astype(bf16)
        near[h] = both(tile(ten.me, seq.me, h), ring)
    for h, other in seconds:
        wide[h] = [both(tile(ten.me, seq.me, h), other)]
    for h, ring in firsts:
        near[h][0].wait_recv()
        far[h] = [hop(tile(*where_of(h, 3), h, 0), ring.next)]
        near[h][1].wait_recv()
        far[h].append(hop(tile(*where_of(h, 1), h, 1), ring.prev))
    for step in (3, 1):
        for h, other in seconds:
            wide[h].append(both(tile(*where_of(h, step), h), other))
    for h, other in seconds:
        far[h][0].wait_recv()
        far[h][1].wait_recv()
        wide[h].append(both(tile(*where_of(h, 2), h), other))
    for i, step in enumerate((0, 3, 1, 2)):
        for h, other in seconds:
            t, s = where_of(h, step)
            across = (lambda k: (other.at(k), s)) if h == 0 else (lambda k: (t, other.at(k)))
            wide[h][i][0].wait_recv()
            last.append(hop(tile(*across(3), h, 0), other.next))
            wide[h][i][1].wait_recv()
            last.append(hop(tile(*across(1), h, 1), other.prev))
    for copy in last:
        copy.wait_recv()

    order = (2, 1, 3, 0)
    place = {step: i for i, step in enumerate(order)}
    both_rows = 2 * rows

    def norm(i):
        base = seq.at(order[i]) * rows

        @pl.loop(0, rows // 16)
        def _(j):
            wide = stream[pl.ds(pl.multiple_of(base + j * 16, 16), 16), :].astype(f32)
            mean = jnp.sum(wide * wide, axis=1, keepdims=True) / features
            normed[pl.ds(pl.multiple_of(i * rows + j * 16, 16), 16), :] = (
                wide * lax.rsqrt(mean + epsilon) * gain_ref[...]
            ).astype(bf16)

        at = pl.ds(i * rows, rows)
        logits = dot(normed[at, :], router_ref[...], TURNED)
        delta = delta_ref[span(seq.at(order[i]), rows), 0:logits.shape[1]]
        side = delta[:, 0:1]
        gap = jnp.sum(delta * logits, axis=1, keepdims=True) * side
        combine[at, :] = jnp.broadcast_to(
            jnp.where(side == 0.0, 0.0, jax.nn.sigmoid(gap)), (rows, combine.shape[1])
        )

    def gate(j):
        at = pl.ds(j * both_rows, both_rows)
        value = dot(normed[at, :], w_gate[...], TURNED)
        hidden[...] = value / (1.0 + jnp.exp(-value)) * combine[at, 0:1]

    def upward(j):
        at = pl.ds(j * both_rows, both_rows)
        hidden[...] = hidden[...] * dot(normed[at, :], w_up[...], TURNED)

    def down(j, first, count):
        at = pl.ds(j * both_rows, both_rows)

        @pl.loop(first, first + count)
        def _(n):
            across = span(n, 512)
            mixed[at, across] = dot(hidden[...].astype(bf16), w_down[:, across], PLAIN).astype(bf16)

    widths = (slots_y.shape[-1], slots_x.shape[-1])
    starts = (0, 2 * widths[0])

    def term(i, col, h, q):
        at = pl.multiple_of(col * cols + starts[h] + q * widths[h], 128)
        return mixed.at[pl.ds(i * rows, rows), pl.ds(at, widths[h])]

    y = [
        RingSum(c, ten, lambda k, q, i=i: term(i, ten.at(k), 0, q), slots_y.at[i])
        for i in range(RING)
    ]
    x = [
        RingSum(c, seq, lambda k, q, i=i: term(place[k], ten.at(order[i]), 1, q), slots_x.at[i])
        for i in range(RING)
    ]
    final = [
        RingSum(c, ring, lambda k, q, h=h, sums=sums: sums.at[place[k], :, pl.ds(q * widths[h], widths[h])], late)
        for h, ring, sums, late in ((0, seq, sums_y, late_y), (1, ten, sums_x, late_x))
    ]

    def settle(h, i):
        source, sums = (y, sums_y) if h == 0 else (x, sums_x)
        for q in range(2):
            sums[i, :, q * widths[h]:(q + 1) * widths[h]] = source[i].total(q).astype(bf16)

    blocks = features // 512
    norm(0)
    norm(1)
    for load in loads:
        load.wait()
    gate(0)
    upward(0)
    down(0, 0, blocks)
    y[0].raw()
    y[1].raw()
    norm(2)
    norm(3)
    y[0].middle()
    gate(1)
    y[1].middle()
    upward(1)
    settle(0, 0)
    final[0].far()
    down(1, 0, blocks)
    y[2].raw()
    x[0].raw()
    y[3].raw()
    x[1].raw()
    settle(0, 1)
    final[0].ahead()
    x[0].middle()
    x[2].raw()
    y[2].middle()
    x[1].middle()
    x[3].raw()
    y[3].middle()
    x[2].middle()
    settle(1, 0)
    final[1].far()
    settle(0, 2)
    final[0].behind()
    final[0].middle()
    x[3].middle()
    settle(1, 1)
    final[1].ahead()
    settle(1, 2)
    final[1].behind()
    final[1].middle()
    settle(0, 3)
    settle(1, 3)
    sent, passed = [], []
    for h in range(2):
        for q in range(2):
            at = starts[h] + q * widths[h]
            own = stream[span(seq.me, rows), pl.ds(pl.multiple_of(ten.me * cols + at, 128), widths[h])]
            packed[span(seq.me, rows), at:at + widths[h]] = (
                own.astype(f32) + final[h].total(q)
            ).astype(bf16)
        sent.append(both(packed.at[span(seq.me, rows), pl.ds(starts[h], 2 * widths[h])], seq))
    for h in range(2):
        sent[h][0].wait_recv()
        passed.append(hop(packed.at[span(seq.at(3), rows), pl.ds(starts[h], widths[h])], seq.next))
        sent[h][1].wait_recv()
        passed.append(hop(packed.at[span(seq.at(1), rows), pl.ds(starts[h] + widths[h], widths[h])], seq.prev))
    for copy in passed:
        copy.wait_recv()
    query = lax.broadcasted_iota(jnp.int32, (out_ref.shape[0], 1), 0) + seq.me * out_ref.shape[0]
    spread = jnp.where(lane_ref[0:1, :] == query, 1.0, 0.0).astype(bf16)
    out_ref[...] = dot(spread, packed[...], PLAIN).astype(bf16)
    c.drain()


def packed_layer(slots, part, own, delta, lane, gain, router, w_gate, w_up, w_down):
    size, cols = part.shape
    features = gain.shape[1]
    units = w_gate.shape[0]
    rows = size // RING
    wide, slim = 3 * cols // 8, cols // 8
    count = 6 + 40 + 60 + 8
    vmem = pl.BlockSpec(memory_space=VMEM)
    hbm = pl.BlockSpec(memory_space=pltpu.HBM)
    dma = pltpu.SemaphoreType.DMA
    return pl.pallas_call(
        layer_kernel,
        out_shape=jax.ShapeDtypeStruct((slots // RING, cols), bf16),
        in_specs=[vmem] * 6 + [hbm] * 3,
        out_specs=vmem,
        scratch_shapes=[
            VMEM((size, features), bf16),
            VMEM((size, features), bf16),
            VMEM((size, features), bf16),
            VMEM((size // 2, units), f32),
            VMEM((size, 128), f32),
            VMEM((size, cols), bf16),
            VMEM((units, features), bf16),
            VMEM((units, features), bf16),
            VMEM((units, features), bf16),
            VMEM((8, rows, cols // 2), bf16),
            VMEM((RING, 8, rows, wide), bf16),
            VMEM((RING, 8, rows, slim), bf16),
            VMEM((RING, rows, 2 * wide), bf16),
            VMEM((RING, rows, 2 * slim), bf16),
            VMEM((8, rows, wide), bf16),
            VMEM((8, rows, slim), bf16),
            dma((3,)), dma((count,)), dma((count,)),
        ],
        compiler_params=pltpu.CompilerParams(
            collective_id=1, has_side_effects=True, vmem_limit_bytes=56 << 20
        ),
        name="layer",
    )(part, own, delta, lane, gain, router, w_gate, w_up, w_down)


def shards(
    residual, queries, attn_keys, attn_values, lengths, requests, routes,
    out_weight, norm_gain, router, w_gate, w_up, w_down,
):
    part, own, delta, lane, most = attend(
        lax.axis_size("replica"), requests, lengths, routes[0].T,
        queries[0], attn_keys[0], attn_values[0], out_weight, residual[0],
    )
    slots, cols = part.shape
    size = min(WINDOW, slots)
    place = jnp.arange(size, dtype=jnp.int32)[None, :]

    def window(i, out):
        start = jnp.minimum(i * size, slots - size)
        own_start = start + lax.axis_index("tensor") * (size // RING)
        fresh = place + start >= i * size
        lanes = jnp.where(fresh, lax.dynamic_slice(lane, (0, start), (lane.shape[0], size)), -1)
        return out + packed_layer(
            slots,
            lax.dynamic_slice(part, (start, 0), (size, cols)),
            lax.dynamic_slice(own, (own_start, 0), (size // RING, cols)),
            lax.dynamic_slice(delta, (start, 0), (size, delta.shape[1])),
            lanes, norm_gain[None], router.T, w_gate[0], w_up[0], w_down[0],
        )

    out = lax.fori_loop(
        0, lax.div(most[0, 0] + (size - 1), size), window, jnp.zeros((slots // RING, cols), bf16)
    )
    return out[None]


def solution(mesh):
    return jax.shard_map(
        shards,
        mesh=mesh,
        in_specs=(
            P("replica", None, None),
            P("replica", "seq", "tensor"),
            P("replica", "seq", "tensor"),
            P("replica", "seq", "tensor"),
            P("replica", None),
            P("replica", None),
            P("replica", None, None),
            P("tensor", "seq"),
            P(),
            P(),
            P(None, ("seq", "tensor"), None),
            P(None, ("seq", "tensor"), None),
            P(None, ("seq", "tensor"), None),
        ),
        out_specs=P("replica", "seq", "tensor"),
        check_vma=False,
    )
```

time: 192 us -> 162 us (0.84)
  matrix products: 28.4 us -> 0 us
  Pallas kernels: 130 us -> 150 us
  loops' own time: 17 us -> 0.24 us
  other arithmetic: 4.46 us -> 1.96 us
    dot_general x7 -> x0, matrix products: 28.4 us -> none  [dot(): lax.dot_general(a, b, (contract, ((), ())), preferred_element_type=f32)]
    another operation x1, loops' own time: 17 us -> 0.24 us  [shards(): lax.fori_loop(0, lax.div(most[0, 0] + (size - 1), size), window, jnp.zero...]
    pallas_call x2 -> x1, Pallas kernels: 88.1 us -> 104 us  [packed_layer(): pl.pallas_call(layer_kernel, out_shape=jax.ShapeDtypeStruct((slots // RIN...]
    pallas_call x1, Pallas kernels: 42.2 us -> 46.2 us  [attend(): pl.pallas_call(functools.partial(attention_kernel, replicas), out_shape=(...]
    dynamic_slice x2 -> x3, local copies, waits for them, and re-layouts: 1.07 us -> 4.31 us  [the longest x1 2.15 us: window(): lax.dynamic_slice(own, (own_start, 0), (size // RING, cols))]
    reduce_sum x2 -> x0, other arithmetic: 3.11 us -> none  [the longest x1 2.02 us: shards(): jnp.sum(most[0, 0] > jnp.array(sizes[:-1], jnp.int32)).astype(jnp.int32)]
    unnamed x8 -> x6, local copies, waits for them, and re-layouts: 3.64 us -> 0.8 us
where the time goes in v1:
time: 162 us; the launch traced here: 160 us
  Pallas kernels  150 us (93%)
  local copies, waits for them, and re-layouts  6.36 us (4%)
  other arithmetic  1.96 us (1%)
    pallas_call x1, Pallas kernels, packed_layer(): pl.pallas_call(layer_kernel, out_shape=jax.ShapeDtypeStruct((slots // RIN...  104 us
    pallas_call x1, Pallas kernels, attend(): pl.pallas_call(functools.partial(attention_kernel, replicas), out_shape=(...  46.2 us

profile of v1, /device:TPU:32, one launch (start us, length us, event | category | flops | bytes accessed | tf_op | source)
XLA Modules:
  0.0 159.7 jit_solution(11264038301496398403)
XLA Ops:
  0.0 0.0 copy-start.2
  0.0 0.0 copy-start.3
  0.0 46.2 %attend.1 = (bf16[1024,1024]{1,0:T(8,128)(2,1)S(1)}, bf16[1024,1024]{1,0:T(8,128)(2,1)}, f32[1024,128]{1,0:T(8,128)S(1)}, s32[8,1024]{1,0:T(8,128)S(1)}, s32[8,128]{1,0:T(8,128)}) custom-call(s32[1,4]{1,0:T(1,128)} %req_ref.1, s32[1,4]{1,0:T(1,128)} %len_ref.1, s32[2,1024]{1,0:T(2,128)} %bitcast.33, bf16[256,1024]{1,0:T(8,128)(2,1)} %bitcast.29, ...), custom_call_target="tpu_custom_call" | custom-call | tf_op jit(solution)/shard_map/attend/pallas_call | solution.py:294
  46.3 1.2 slice.3
  48.1 0.1 broadcast_in_dim.22
  48.2 0.0 copy-done.2
  48.2 0.0 copy-done.3
  48.2 110.7 %while.11 = (s32[]{:T(128)}, bf16[256,1024]{1,0:T(8,128)(2,1)S(1)}, s32[]{:T(128)}, bf16[1024,1024]{1,0:T(8,128)(2,1)S(1)}, bf16[1024,1024]{1,0:T(8,128)(2,1)}, ...) while((s32[]{:T(128)}, bf16[256,1024]{1,0:T(8,128)(2,1)S(1)}, ...), condition=%wide.region_1.2_spmd.clone, body=%wide.region_0.1_spmd.clone.sunk | while | flops 268558 | bytes 20227688 | solution.py:594
  48.4 0.0 copy-start
  48.4 0.7 dynamic-slice_select_fusion.2.lane_ref
  49.1 2.1 %constant_dynamic-slice_fusion.7.res_ref = bf16[160,1024]{1,0:T(8,128)(2,1)} fusion(bf16[1024,1024]{1,0:T(8,128)(2,1)} %get-tuple-element.251, s32[]{:T(128)S(6)} %select_n.21), kind=kLoop, calls=%fused_computation.5.clone.1 | loop fusion | bytes 655364 | tf_op jit(solution)/shard_map/while/body/dynamic_slice | solution.py:589
  51.3 0.8 constant_dynamic-slice_fusion.8.delta_ref
  52.0 1.4 constant_dynamic-slice_fusion.6.part_ref
  53.4 0.0 copy-done
  53.4 104.2 %layer.1 = bf16[256,1024]{1,0:T(8,128)(2,1)} custom-call(bf16[640,1024]{1,0:T(8,128)(2,1)} %constant_dynamic-slice_fusion.6.part_ref, bf16[160,1024]{1,0:T(8,128)(2,1)} %constant_dynamic-slice_fusion.7.res_ref, f32[640,128]{1,0:T(8,128)} %constant_dynamic-slice_fusion.8.delta_ref, s32[8,640]{1,0:T(8,128)} %dynamic-slice_select_fusion.2.lane_ref, ...), custom_call_target="tpu_custom_call" | custom-call | tf_op jit(solution)/shard_map/while/body/layer/pallas_call | solution.py:538
  157.7 1.3 add.59
  158.9 0.0 copy-start.1
  158.9 0.8 copy-done.1
  (1 shorter events, 0.0 us)
Async XLA Ops:
  0.0 48.2 %copy-start.2 = (bf16[4096,8]{0,1:T(8,128)(2,1)S(1)}, bf16[4096,8]{0,1:T(8,128)(2,1)}, u32[]{:S(2)}) copy-start(bf16[4096,8]{0,1:T(8,128)(2,1)} %param.24) | copy-start | bytes 196612
  0.0 48.2 %copy-start.3 = (f32[4096]{0:T(1024)S(1)}, f32[4096]{0:T(1024)}, u32[]{:S(2)}) copy-start(f32[4096]{0:T(1024)} %param.23) | copy-start | bytes 49156
  48.4 5.0 %copy-start = (bf16[1,448,4096]{2,1,0:T(8,128)(2,1)S(1)}, bf16[1,448,4096]{2,1,0:T(8,128)(2,1)}, u32[]{:S(2)}) copy-start(bf16[1,448,4096]{2,1,0:T(8,128)(2,1)} %get-tuple-element.256) | copy-start | bytes 11010052 | tf_op jit(solution)/shard_map/while
  158.9 0.8 copy-start.1

commit v2 on v1

--- a/solution.py
+++ b/solution.py
@@ -120,7 +120,7 @@
 
 def attention_kernel(
     replicas, req_ref, len_ref, routes_ref, q_hbm, k_hbm, v_hbm, w_hbm, res_hbm,
-    part_ref, own_ref, delta_ref, lane_ref, most_ref,
+    part_ref, own_ref, delta_ref, lane_ref, turns_ref,
     req, every, q_ref, kv, bias, pick, att_ref, w_ref, res_ref, proj,
     local, send, recv, req_send, req_recv,
 ):
@@ -172,7 +172,7 @@
         share = jnp.where(left < 0, share - 1, jnp.where(left >= total, share + 1, share))
         admitted = jnp.where(lane == b, jnp.minimum(wanted, jnp.maximum(1.0, share)), admitted)
     most = jnp.max(jnp.sum(admitted, axis=1, keepdims=True), axis=0, keepdims=True)
-    most_ref[...] = jnp.broadcast_to(most, most_ref.shape).astype(jnp.int32)
+    turns_ref[0] = lax.div(most[0, 0].astype(jnp.int32) + (WINDOW - 1), WINDOW)
     mine = lax.broadcasted_iota(jnp.int32, wanted.shape, 0) == me
     row = jnp.sum(jnp.where(mine, admitted, 0.0), axis=0, keepdims=True)
     lane_one = lax.broadcasted_iota(jnp.int32, row.shape, 1)
@@ -228,22 +228,24 @@
     loads[2].wait()
 
     scale = 1.0 / math.sqrt(HEAD_DIM)
-    span_g = group * HEAD_DIM
+    pair = 2 * HEAD_DIM
+    pairs = q_ref.shape[1] // pair
     sent = []
-    for g in range(kv_count):
+    for p in range(pairs):
+        g = 2 * p // group
         keys = kv[:, :, g * HEAD_DIM:(g + 1) * HEAD_DIM].reshape(slots, HEAD_DIM)
         values = kv[:, :, wide + g * HEAD_DIM:wide + (g + 1) * HEAD_DIM].reshape(slots, HEAD_DIM)
 
-        @pl.loop(0, group)
+        @pl.loop(2 * p, 2 * p + 2)
         def _(h):
-            at = span(h + g * group, HEAD_DIM)
+            at = span(h, HEAD_DIM)
             scores = dot(q_ref[:, at], keys, TURNED) * scale + bias[...]
             highest = jnp.max(scores, axis=1, keepdims=True)
             weights = jnp.exp(scores - highest).astype(bf16)
             norm = jnp.sum(weights.astype(f32), axis=1, keepdims=True)
             att_ref[span(seq.me, rows), at] = (dot(weights, values, PLAIN) / norm).astype(bf16)
 
-        mine = att_ref.at[span(seq.me, rows), pl.ds(g * span_g, span_g)]
+        mine = att_ref.at[span(seq.me, rows), pl.ds(p * pair, pair)]
         sent.append((c.start(mine, mine, seq.next), c.start(mine, mine, seq.prev)))
 
     def project(block, start):
@@ -265,13 +267,12 @@
     loads[4].wait()
     project(seq.me, True)
     passed = []
-    part = span_g // 2
-    for g in range(kv_count):
-        sent[g][0].wait_recv()
-        there = att_ref.at[span(seq.at(3), rows), pl.ds(g * span_g, part)]
+    for p in range(pairs):
+        sent[p][0].wait_recv()
+        there = att_ref.at[span(seq.at(3), rows), pl.ds(p * pair, HEAD_DIM)]
         passed.append(c.start(there, there, seq.next))
-        sent[g][1].wait_recv()
-        there = att_ref.at[span(seq.at(1), rows), pl.ds(g * span_g + part, part)]
+        sent[p][1].wait_recv()
+        there = att_ref.at[span(seq.at(1), rows), pl.ds(p * pair + HEAD_DIM, HEAD_DIM)]
         passed.append(c.start(there, there, seq.prev))
     project(seq.at(3), False)
     project(seq.at(1), False)
@@ -286,8 +287,7 @@
     rows, heads = queries.shape
     slots = RING * rows
     cols = out_weight.shape[1]
-    groups = keys.shape[1] // HEAD_DIM
-    count = 4 + 4 * groups
+    count = 4 + 4 * (heads // (2 * HEAD_DIM))
     vmem = pl.BlockSpec(memory_space=VMEM)
     hbm = pl.BlockSpec(memory_space=pltpu.HBM)
     dma = pltpu.SemaphoreType.DMA
@@ -298,10 +298,10 @@
             jax.ShapeDtypeStruct((slots, cols), bf16),
             jax.ShapeDtypeStruct((slots, 128), f32),
             jax.ShapeDtypeStruct((8, slots), jnp.int32),
-            jax.ShapeDtypeStruct((8, 128), jnp.int32),
+            jax.ShapeDtypeStruct((1,), jnp.int32),
         ),
         in_specs=[vmem] * 3 + [hbm] * 5,
-        out_specs=(vmem,) * 5,
+        out_specs=(vmem,) * 4 + (pl.BlockSpec(memory_space=pltpu.SMEM),),
         scratch_shapes=[
             VMEM((8, 128), f32),
             VMEM((replicas, 8, 128), f32),
@@ -316,20 +316,22 @@
             dma((5,)), dma((count,)), dma((count,)), dma((replicas - 1,)), dma((replicas - 1,)),
         ],
         compiler_params=pltpu.CompilerParams(
-            collective_id=0, has_side_effects=True, vmem_limit_bytes=58 << 20
+            collective_id=0, has_side_effects=True, vmem_limit_bytes=57 << 20
         ),
         name="attend",
     )(requests, lengths, routes, queries, keys, values, out_weight, residual)
 
 
 def layer_kernel(
-    part_ref, res_ref, delta_ref, lane_ref, gain_ref, router_ref, gate_hbm, up_hbm, down_hbm,
+    turn_ref, part_ref, res_ref, delta_ref, lane_ref, before_ref, gain_ref, router_ref,
+    gate_hbm, up_hbm, down_hbm,
     out_ref,
-    stream, mixed, normed, hidden, combine, packed, w_gate, w_up, w_down,
+    terms, stream, mixed, scaled, squares, hidden, share, units, packed, w_gate, w_up, w_down,
     slots_c, slots_y, slots_x, sums_y, sums_x, late_y, late_x, local, send, recv,
 ):
     seq, ten = Ring("seq"), Ring("tensor")
-    rows, cols = res_ref.shape
+    size, cols = terms.shape
+    rows = size // RING
     features = stream.shape[1]
     half, quarter = cols // 2, cols // 4
     loads = [
@@ -347,10 +349,26 @@
     def hop(ref, where):
         return c.start(ref, ref, where)
 
+    slots = part_ref.shape[0]
+    begins = [min(w * size, slots - size) for w in range(-(-slots // size))]
+    turn = jnp.full((1, 1), turn_ref[0], jnp.int32)
+
+    def chosen(read):
+        value = read(begins[0]).astype(f32)
+        for w, begin in enumerate(begins[1:], 1):
+            value = jnp.where(turn == w, read(begin).astype(f32), value)
+        return value
+
+    def window(index, begin):
+        return pl.ds(pl.multiple_of(begin + index * rows, math.gcd(begin, rows)), rows)
+
     summed = RingSum(
-        c, ten, lambda k, h: part_ref.at[span(ten.at(k), rows), pl.ds(h * half, half)], slots_c
+        c, ten, lambda k, h: terms.at[span(ten.at(k), rows), pl.ds(h * half, half)], slots_c
     )
+    for k in range(RING):
+        terms[k * rows:(k + 1) * rows, :] = chosen(lambda begin: part_ref[window(k, begin), :]).astype(bf16)
     summed.raw()
+    squares[...] = jnp.zeros_like(squares)
     summed.middle()
 
     def tile(t, s, h, q=None):
@@ -359,16 +377,36 @@
 
     def where_of(h, step):
         return (ten.me, seq.at(step)) if h == 0 else (ten.at(step), seq.me)
+
+    order = (2, 1, 3, 0)
+    place = {step: i for i, step in enumerate(order)}
+    both_rows = 2 * rows
+
+    def take(t, s, h):
+        base = t * rows
+        at = pl.ds(pl.multiple_of(s * cols + h * half, half), half)
+        gain = gain_ref[:, at]
+
+        @pl.loop(0, rows // 32)
+        def _(j):
+            here = pl.ds(pl.multiple_of(base + j * 32, 32), 32)
+            values = stream[here, at].astype(f32)
+            squares[here, :] += jnp.broadcast_to(
+                jnp.sum(values * values, axis=1, keepdims=True), (32, squares.shape[1])
+            )
+            scaled[here, at] = (values * gain).astype(bf16)
 
     firsts, seconds = ((0, seq), (1, ten)), ((0, ten), (1, seq))
     near, wide, far, last = {}, {}, {}, []
     for h, ring in firsts:
         tile(ten.me, seq.me, h)[...] = (
-            res_ref[:, h * half:(h + 1) * half].astype(f32) + summed.total(h)
+            chosen(lambda begin: res_ref[window(ten.me, begin), h * half:(h + 1) * half]) + summed.total(h)
         ).astype(bf16)
         near[h] = both(tile(ten.me, seq.me, h), ring)
     for h, other in seconds:
         wide[h] = [both(tile(ten.me, seq.me, h), other)]
+    for h in range(2):
+        take(ten.me, seq.me, h)
     for h, ring in firsts:
         near[h][0].wait_recv()
         far[h] = [hop(tile(*where_of(h, 3), h, 0), ring.next)]
@@ -377,61 +415,67 @@
     for step in (3, 1):
         for h, other in seconds:
             wide[h].append(both(tile(*where_of(h, step), h), other))
+    for step in (3, 1):
+        for h in range(2):
+            take(*where_of(h, step), h)
     for h, other in seconds:
         far[h][0].wait_recv()
         far[h][1].wait_recv()
         wide[h].append(both(tile(*where_of(h, 2), h), other))
+    for h in range(2):
+        take(*where_of(h, 2), h)
     for i, step in enumerate((0, 3, 1, 2)):
+        arrived = []
         for h, other in seconds:
             t, s = where_of(h, step)
-            across = (lambda k: (other.at(k), s)) if h == 0 else (lambda k: (t, other.at(k)))
+            across = [(other.at(k), s) if h == 0 else (t, other.at(k)) for k in range(RING)]
             wide[h][i][0].wait_recv()
-            last.append(hop(tile(*across(3), h, 0), other.next))
+            one = hop(tile(*across[3], h, 0), other.next)
             wide[h][i][1].wait_recv()
-            last.append(hop(tile(*across(1), h, 1), other.prev))
-    for copy in last:
-        copy.wait_recv()
-
-    order = (2, 1, 3, 0)
-    place = {step: i for i, step in enumerate(order)}
-    both_rows = 2 * rows
-
-    def norm(i):
-        base = seq.at(order[i]) * rows
-
-        @pl.loop(0, rows // 16)
-        def _(j):
-            wide = stream[pl.ds(pl.multiple_of(base + j * 16, 16), 16), :].astype(f32)
-            mean = jnp.sum(wide * wide, axis=1, keepdims=True) / features
-            normed[pl.ds(pl.multiple_of(i * rows + j * 16, 16), 16), :] = (
-                wide * lax.rsqrt(mean + epsilon) * gain_ref[...]
-            ).astype(bf16)
-
-        at = pl.ds(i * rows, rows)
-        logits = dot(normed[at, :], router_ref[...], TURNED)
-        delta = delta_ref[span(seq.at(order[i]), rows), 0:logits.shape[1]]
+            two = hop(tile(*across[1], h, 1), other.prev)
+            last.append((one, two, (*across[2], h)))
+            arrived += [(*across[3], h), (*across[1], h)]
+        for which in arrived:
+            take(*which)
+    for one, two, which in last:
+        one.wait_recv()
+        two.wait_recv()
+        take(*which)
+    for load in loads:
+        load.wait()
+
+    def weigh(i):
+        here = span(seq.at(order[i]), rows)
+        factor = lax.rsqrt(squares[here, 0:1] / features + epsilon)
+        logits = dot(scaled[here, :], router_ref[...], TURNED) * factor
+        delta = chosen(lambda begin: delta_ref[window(seq.at(order[i]), begin), 0:logits.shape[1]])
         side = delta[:, 0:1]
         gap = jnp.sum(delta * logits, axis=1, keepdims=True) * side
-        combine[at, :] = jnp.broadcast_to(
-            jnp.where(side == 0.0, 0.0, jax.nn.sigmoid(gap)), (rows, combine.shape[1])
+        weight = jnp.where(side == 0.0, 0.0, jax.nn.sigmoid(gap))
+        units[0, i * rows:(i + 1) * rows, :] = jnp.broadcast_to(factor, (rows, units.shape[2]))
+        units[1, i * rows:(i + 1) * rows, :] = jnp.broadcast_to(weight * factor, (rows, units.shape[2]))
+
+    def pair(j):
+        return jnp.concatenate(
+            [scaled[span(seq.at(order[i]), rows), :] for i in (2 * j, 2 * j + 1)], axis=0
         )
 
     def gate(j):
         at = pl.ds(j * both_rows, both_rows)
-        value = dot(normed[at, :], w_gate[...], TURNED)
-        hidden[...] = value / (1.0 + jnp.exp(-value)) * combine[at, 0:1]
+        value = dot(pair(j), w_gate[...], TURNED) * units[0, at, 0:1]
+        hidden[...] = value / (1.0 + jnp.exp(-value)) * units[1, at, 0:1]
 
     def upward(j):
+        value = hidden[...] * dot(pair(j), w_up[...], TURNED)
+        share[...] = value.astype(bf16)
+
+    def down(j):
         at = pl.ds(j * both_rows, both_rows)
-        hidden[...] = hidden[...] * dot(normed[at, :], w_up[...], TURNED)
-
-    def down(j, first, count):
-        at = pl.ds(j * both_rows, both_rows)
-
-        @pl.loop(first, first + count)
+
+        @pl.loop(0, features // 1024)
         def _(n):
-            across = span(n, 512)
-            mixed[at, across] = dot(hidden[...].astype(bf16), w_down[:, across], PLAIN).astype(bf16)
+            across = span(n, 1024)
+            mixed[at, across] = dot(share[...], w_down[:, across], PLAIN).astype(bf16)
 
     widths = (slots_y.shape[-1], slots_x.shape[-1])
     starts = (0, 2 * widths[0])
@@ -458,25 +502,22 @@
         for q in range(2):
             sums[i, :, q * widths[h]:(q + 1) * widths[h]] = source[i].total(q).astype(bf16)
 
-    blocks = features // 512
-    norm(0)
-    norm(1)
-    for load in loads:
-        load.wait()
+    weigh(0)
+    weigh(1)
     gate(0)
     upward(0)
-    down(0, 0, blocks)
+    down(0)
     y[0].raw()
     y[1].raw()
-    norm(2)
-    norm(3)
+    weigh(2)
+    weigh(3)
     y[0].middle()
     gate(1)
     y[1].middle()
     upward(1)
     settle(0, 0)
     final[0].far()
-    down(1, 0, blocks)
+    down(1)
     y[2].raw()
     x[0].raw()
     y[3].raw()
@@ -520,13 +561,18 @@
     for copy in passed:
         copy.wait_recv()
     query = lax.broadcasted_iota(jnp.int32, (out_ref.shape[0], 1), 0) + seq.me * out_ref.shape[0]
-    spread = jnp.where(lane_ref[0:1, :] == query, 1.0, 0.0).astype(bf16)
-    out_ref[...] = dot(spread, packed[...], PLAIN).astype(bf16)
+    slot = lane_ref[0:1, 0:size]
+    for w, begin in enumerate(begins[1:], 1):
+        row = lax.broadcasted_iota(jnp.int32, slot.shape, 1) + begin
+        later = jnp.where(row >= w * size, lane_ref[0:1, begin:begin + size], -1)
+        slot = jnp.where(turn == w, later, slot)
+    spread = jnp.where(slot == query, 1.0, 0.0).astype(bf16)
+    out_ref[...] = (before_ref[...].astype(f32) + dot(spread, packed[...], PLAIN)).astype(bf16)
     c.drain()
 
 
-def packed_layer(slots, part, own, delta, lane, gain, router, w_gate, w_up, w_down):
-    size, cols = part.shape
+def packed_layer(size, turn, part, own, delta, lane, before, gain, router, w_gate, w_up, w_down):
+    cols = part.shape[1]
     features = gain.shape[1]
     units = w_gate.shape[0]
     rows = size // RING
@@ -537,15 +583,18 @@
     dma = pltpu.SemaphoreType.DMA
     return pl.pallas_call(
         layer_kernel,
-        out_shape=jax.ShapeDtypeStruct((slots // RING, cols), bf16),
-        in_specs=[vmem] * 6 + [hbm] * 3,
+        out_shape=jax.ShapeDtypeStruct(before.shape, bf16),
+        in_specs=[pl.BlockSpec(memory_space=pltpu.SMEM)] + [vmem] * 7 + [hbm] * 3,
         out_specs=vmem,
         scratch_shapes=[
+            VMEM((size, cols), bf16),
             VMEM((size, features), bf16),
             VMEM((size, features), bf16),
             VMEM((size, features), bf16),
+            VMEM((size, 128), f32),
             VMEM((size // 2, units), f32),
-            VMEM((size, 128), f32),
+            VMEM((size // 2, units), bf16),
+            VMEM((2, size, 128), f32),
             VMEM((size, cols), bf16),
             VMEM((units, features), bf16),
             VMEM((units, features), bf16),
@@ -563,37 +612,26 @@
             collective_id=1, has_side_effects=True, vmem_limit_bytes=56 << 20
         ),
         name="layer",
-    )(part, own, delta, lane, gain, router, w_gate, w_up, w_down)
+    )(turn, part, own, delta, lane, before, gain, router, w_gate, w_up, w_down)
 
 
 def shards(
     residual, queries, attn_keys, attn_values, lengths, requests, routes,
     out_weight, norm_gain, router, w_gate, w_up, w_down,
 ):
-    part, own, delta, lane, most = attend(
+    part, own, delta, lane, turns = attend(
         lax.axis_size("replica"), requests, lengths, routes[0].T,
         queries[0], attn_keys[0], attn_values[0], out_weight, residual[0],
     )
     slots, cols = part.shape
-    size = min(WINDOW, slots)
-    place = jnp.arange(size, dtype=jnp.int32)[None, :]
-
-    def window(i, out):
-        start = jnp.minimum(i * size, slots - size)
-        own_start = start + lax.axis_index("tensor") * (size // RING)
-        fresh = place + start >= i * size
-        lanes = jnp.where(fresh, lax.dynamic_slice(lane, (0, start), (lane.shape[0], size)), -1)
-        return out + packed_layer(
-            slots,
-            lax.dynamic_slice(part, (start, 0), (size, cols)),
-            lax.dynamic_slice(own, (own_start, 0), (size // RING, cols)),
-            lax.dynamic_slice(delta, (start, 0), (size, delta.shape[1])),
-            lanes, norm_gain[None], router.T, w_gate[0], w_up[0], w_down[0],
+
+    def window(turn, out):
+        return packed_layer(
+            min(WINDOW, slots), turn[None], part, own, delta, lane, out,
+            norm_gain[None], router.T, w_gate[0], w_up[0], w_down[0],
         )
 
-    out = lax.fori_loop(
-        0, lax.div(most[0, 0] + (size - 1), size), window, jnp.zeros((slots // RING, cols), bf16)
-    )
+    out = lax.fori_loop(0, turns[0], window, jnp.zeros((slots // RING, cols), bf16))
     return out[None]
 
 

time: 162 us -> 150 us (0.926)
  Pallas kernels: 150 us -> 145 us
  local copies, waits for them, and re-layouts: 6.36 us -> 1.65 us
  other arithmetic: 1.96 us -> 0 us
    pallas_call x1, Pallas kernels: 104 us -> 99.9 us  [packed_layer(): pl.pallas_call(layer_kernel, out_shape=jax.ShapeDtypeStruct(before.shape,...]
    dynamic_slice x3 -> x0, local copies, waits for them, and re-layouts: 4.31 us -> none  [the longest x1 2.15 us: window(): lax.dynamic_slice(own, (own_start, 0), (size // RING, cols))]
where the time goes in v2:
time: 150 us; the launch traced here: 148 us
  Pallas kernels  145 us (97%)
  local copies, waits for them, and re-layouts  1.65 us (1%)
    pallas_call x1, Pallas kernels, packed_layer(): pl.pallas_call(layer_kernel, out_shape=jax.ShapeDtypeStruct(before.shape,...  99.9 us
    pallas_call x1, Pallas kernels, attend(): pl.pallas_call(functools.partial(attention_kernel, replicas), out_shape=(...  45 us

profile of v2, /device:TPU:32, one launch (start us, length us, event | category | flops | bytes accessed | tf_op | source)
XLA Modules:
  0.0 148.0 jit_solution(5455767912803052054)
XLA Ops:
  0.0 0.0 copy-start
  0.0 0.0 copy-start.1
  0.0 45.0 %attend.1 = (bf16[1024,1024]{1,0:T(8,128)(2,1)S(1)}, bf16[1024,1024]{1,0:T(8,128)(2,1)}, f32[1024,128]{1,0:T(8,128)S(1)}, s32[8,1024]{1,0:T(8,128)S(1)}, s32[1]{0:T(128)}) custom-call(s32[1,4]{1,0:T(1,128)} %req_ref.1, s32[1,4]{1,0:T(1,128)} %len_ref.1, s32[2,1024]{1,0:T(2,128)} %bitcast.37, bf16[256,1024]{1,0:T(8,128)(2,1)} %bitcast.33, ...), custom_call_target="tpu_custom_call" | custom-call | tf_op jit(solution)/shard_map/attend/pallas_call | solution.py:294
  45.0 0.1 broadcast_in_dim.12
  45.1 0.0 copy-done
  45.1 0.0 copy-done.1
  45.1 102.1 %while.10 = (s32[]{:T(128)}, bf16[256,1024]{1,0:T(8,128)(2,1)S(1)}, s32[]{:T(128)}, f32[4096]{0:T(1024)S(1)}, bf16[4096,8]{0,1:T(8,128)(2,1)S(1)}, /*index=5*/bf...) while((s32[]{:T(128)}, bf16[256,1024]{1,0:T(8,128)(2,1)S(1)}, ...), condition=%wide.region_1.0_spmd, body=%wide.region_0.0_spmd.sunk | while | flops 2 | bytes 1048709 | solution.py:634
  45.9 0.8 copy.24.before_ref
  46.7 99.9 %layer.1 = bf16[256,1024]{1,0:T(8,128)(2,1)S(1)} custom-call(s32[1]{0:T(128)} %bitcast.21.turn_ref, bf16[1024,1024]{1,0:T(8,128)(2,1)S(1)} %get-tuple-element.211.part_ref, bf16[1024,1024]{1,0:T(8,128)(2,1)} %get-tuple-element.212.res_ref, f32[1024,128]{1,0:T(8,128)S(1)} %get-tuple-element.213.delta_ref, s32[8,1024]{1,0:T(8,128)S(1)} %get-tuple-element.214.lane_ref, ...), custom_call_target="tpu_custom_call" | custom-call | tf_op jit(solution)/shard_map/while/body/layer/pallas_call | solution.py:584
  147.2 0.8 copy.25
Async XLA Ops:
  0.0 45.1 %copy-start = (bf16[4096,8]{0,1:T(8,128)(2,1)S(1)}, bf16[4096,8]{0,1:T(8,128)(2,1)}, u32[]{:S(2)}) copy-start(bf16[4096,8]{0,1:T(8,128)(2,1)} %param.24) | copy-start | bytes 196612
  0.0 45.1 %copy-start.1 = (f32[4096]{0:T(1024)S(1)}, f32[4096]{0:T(1024)}, u32[]{:S(2)}) copy-start(f32[4096]{0:T(1024)} %param.23) | copy-start | bytes 49156

commit v3 on v2

--- a/solution.py
+++ b/solution.py
@@ -78,6 +78,16 @@
 class RingSum:
     def __init__(self, copies, ring, block, slots):
         self.copies, self.ring, self.block, self.slots = copies, ring, block, slots
+
+    def first(self):
+        c, r, s = self.copies, self.ring, self.slots
+        self.a = c.start(self.block(2, 0), s.at[0], r.next)
+        self.behind()
+
+    def second(self):
+        c, r, s = self.copies, self.ring, self.slots
+        self.b = c.start(self.block(2, 1), s.at[1], r.prev)
+        self.ahead()
 
     def far(self):
         c, r, s = self.copies, self.ring, self.slots
@@ -327,7 +337,7 @@
     gate_hbm, up_hbm, down_hbm,
     out_ref,
     terms, stream, mixed, scaled, squares, hidden, share, units, packed, w_gate, w_up, w_down,
-    slots_c, slots_y, slots_x, sums_y, sums_x, late_y, late_x, local, send, recv,
+    slots_c, slots_y, slots_e, slots_x, sums_x, late_x, spread, laid, base, tail, local, send, recv,
 ):
     seq, ten = Ring("seq"), Ring("tensor")
     size, cols = terms.shape
@@ -383,13 +393,13 @@
     both_rows = 2 * rows
 
     def take(t, s, h):
-        base = t * rows
+        first = t * rows
         at = pl.ds(pl.multiple_of(s * cols + h * half, half), half)
         gain = gain_ref[:, at]
 
         @pl.loop(0, rows // 32)
         def _(j):
-            here = pl.ds(pl.multiple_of(base + j * 32, 32), 32)
+            here = pl.ds(pl.multiple_of(first + j * 32, 32), 32)
             values = stream[here, at].astype(f32)
             squares[here, :] += jnp.broadcast_to(
                 jnp.sum(values * values, axis=1, keepdims=True), (32, squares.shape[1])
@@ -405,6 +415,17 @@
         near[h] = both(tile(ten.me, seq.me, h), ring)
     for h, other in seconds:
         wide[h] = [both(tile(ten.me, seq.me, h), other)]
+    slot = lane_ref[0:1, 0:size]
+    for w, begin in enumerate(begins[1:], 1):
+        row = lax.broadcasted_iota(jnp.int32, slot.shape, 1) + begin
+        later = jnp.where(row >= w * size, lane_ref[0:1, begin:begin + size], -1)
+        slot = jnp.where(turn == w, later, slot)
+
+    @pl.loop(0, slots // 128)
+    def _(i):
+        here = lax.broadcasted_iota(jnp.int32, (128, 1), 0) + i * 128
+        spread[span(i, 128), :] = jnp.where(slot == here, 1.0, 0.0).astype(bf16)
+
     for h in range(2):
         take(ten.me, seq.me, h)
     for h, ring in firsts:
@@ -445,129 +466,153 @@
         load.wait()
 
     def weigh(i):
-        here = span(seq.at(order[i]), rows)
+        here = pl.ds(i * rows, rows)
         factor = lax.rsqrt(squares[here, 0:1] / features + epsilon)
         logits = dot(scaled[here, :], router_ref[...], TURNED) * factor
-        delta = chosen(lambda begin: delta_ref[window(seq.at(order[i]), begin), 0:logits.shape[1]])
+        delta = chosen(lambda begin: delta_ref[window(i, begin), 0:logits.shape[1]])
         side = delta[:, 0:1]
         gap = jnp.sum(delta * logits, axis=1, keepdims=True) * side
         weight = jnp.where(side == 0.0, 0.0, jax.nn.sigmoid(gap))
-        units[0, i * rows:(i + 1) * rows, :] = jnp.broadcast_to(factor, (rows, units.shape[2]))
-        units[1, i * rows:(i + 1) * rows, :] = jnp.broadcast_to(weight * factor, (rows, units.shape[2]))
-
-    def pair(j):
-        return jnp.concatenate(
-            [scaled[span(seq.at(order[i]), rows), :] for i in (2 * j, 2 * j + 1)], axis=0
+        units[0, here, :] = jnp.broadcast_to(factor, (rows, units.shape[2]))
+        units[1, here, :] = jnp.broadcast_to(weight * factor, (rows, units.shape[2]))
+
+    def work(j):
+        at = pl.ds(j * both_rows, both_rows)
+        value = dot(scaled[at, :], w_gate[...], TURNED) * units[0, at, 0:1]
+        hidden[...] = value / (1.0 + jnp.exp(-value)) * units[1, at, 0:1]
+        share[at, :] = (hidden[...] * dot(scaled[at, :], w_up[...], TURNED)).astype(bf16)
+
+    def down(j, at):
+        @pl.loop(0, RING)
+        def _(n):
+            across = pl.ds(pl.multiple_of(n * cols + j * half, half), half)
+            mixed[at, across] = dot(share[at, :], w_down[:, across], PLAIN).astype(bf16)
+
+    def share_of(col, start, width):
+        return pl.ds(pl.multiple_of(col * cols + start, 128), width)
+
+    slim = tail.shape[1]
+    widths = (quarter, quarter, half - slim)
+    y = [
+        RingSum(
+            c, ten,
+            lambda k, q, j=j: mixed.at[
+                pl.ds(q * both_rows, both_rows), share_of(ten.at(k), j * quarter, widths[j])
+            ],
+            slots_y.at[j, :, :, pl.ds(0, widths[j])],
         )
-
-    def gate(j):
-        at = pl.ds(j * both_rows, both_rows)
-        value = dot(pair(j), w_gate[...], TURNED) * units[0, at, 0:1]
-        hidden[...] = value / (1.0 + jnp.exp(-value)) * units[1, at, 0:1]
-
-    def upward(j):
-        value = hidden[...] * dot(pair(j), w_up[...], TURNED)
-        share[...] = value.astype(bf16)
-
-    def down(j):
-        at = pl.ds(j * both_rows, both_rows)
-
-        @pl.loop(0, features // 1024)
-        def _(n):
-            across = span(n, 1024)
-            mixed[at, across] = dot(share[...], w_down[:, across], PLAIN).astype(bf16)
-
-    widths = (slots_y.shape[-1], slots_x.shape[-1])
-    starts = (0, 2 * widths[0])
-
-    def term(i, col, h, q):
-        at = pl.multiple_of(col * cols + starts[h] + q * widths[h], 128)
-        return mixed.at[pl.ds(i * rows, rows), pl.ds(at, widths[h])]
-
-    y = [
-        RingSum(c, ten, lambda k, q, i=i: term(i, ten.at(k), 0, q), slots_y.at[i])
+        for j in range(3)
+    ]
+    part_rows = out_ref.shape[0] // 2
+    e = [
+        RingSum(
+            c, seq,
+            lambda k, q, j=j: laid.at[
+                j, pl.ds(pl.multiple_of(seq.at(k) * (2 * part_rows) + q * part_rows, part_rows), part_rows),
+                pl.ds(0, widths[j]),
+            ],
+            slots_e.at[j, :, :, pl.ds(0, widths[j])],
+        )
+        for j in range(3)
+    ]
+
+    def lay(j):
+        for q in range(2):
+            packed[q * both_rows:(q + 1) * both_rows, 0:widths[j]] = y[j].total(q).astype(bf16)
+
+        @pl.loop(0, RING)
+        def _(i):
+            laid[j, span(i, 2 * part_rows), 0:widths[j]] = dot(
+                spread[span(i, 2 * part_rows), :], packed[:, 0:widths[j]], PLAIN
+            ).astype(bf16)
+
+        e[j].raw()
+
+    def write(j):
+        at = slice(j * quarter, j * quarter + widths[j])
+        for q in range(2):
+            here = slice(q * part_rows, (q + 1) * part_rows)
+            out_ref[here, at] = (base[here, at] + e[j].total(q)).astype(bf16)
+
+    few = rows // 2
+
+    def half_of(index, q):
+        return pl.ds(pl.multiple_of(index * rows + q * few, few), few)
+
+    x = [
+        RingSum(
+            c, seq,
+            lambda k, q, i=i: mixed.at[half_of(seq.at(k), q), share_of(ten.at(order[i]), cols - slim, slim)],
+            slots_x.at[i],
+        )
         for i in range(RING)
     ]
-    x = [
-        RingSum(c, seq, lambda k, q, i=i: term(place[k], ten.at(order[i]), 1, q), slots_x.at[i])
-        for i in range(RING)
-    ]
-    final = [
-        RingSum(c, ring, lambda k, q, h=h, sums=sums: sums.at[place[k], :, pl.ds(q * widths[h], widths[h])], late)
-        for h, ring, sums, late in ((0, seq, sums_y, late_y), (1, ten, sums_x, late_x))
-    ]
-
-    def settle(h, i):
-        source, sums = (y, sums_y) if h == 0 else (x, sums_x)
+    final = RingSum(c, ten, lambda k, q: sums_x.at[place[k], pl.ds(q * few, few)], late_x)
+
+    def settle(i):
         for q in range(2):
-            sums[i, :, q * widths[h]:(q + 1) * widths[h]] = source[i].total(q).astype(bf16)
-
+            sums_x[i, q * few:(q + 1) * few, :] = x[i].total(q).astype(bf16)
+
+    above, below = pl.ds(0, both_rows), pl.ds(both_rows, both_rows)
     weigh(0)
     weigh(1)
-    gate(0)
-    upward(0)
-    down(0)
-    y[0].raw()
-    y[1].raw()
+    work(0)
+    down(0, above)
+    y[0].first()
+    y[1].first()
     weigh(2)
     weigh(3)
+    work(1)
+    down(1, pl.ds(0, size))
+    x[0].raw()
+    x[1].raw()
+    down(0, below)
+    y[0].second()
+    y[1].second()
     y[0].middle()
-    gate(1)
-    y[1].middle()
-    upward(1)
-    settle(0, 0)
-    final[0].far()
-    down(1)
     y[2].raw()
-    x[0].raw()
-    y[3].raw()
-    x[1].raw()
-    settle(0, 1)
-    final[0].ahead()
+    own_rows = spread[span(seq.me, 2 * part_rows), :]
+    base[...] = before_ref[...].astype(f32) + dot(
+        own_rows, stream[:, pl.ds(pl.multiple_of(ten.me * cols, cols), cols)], PLAIN
+    )
     x[0].middle()
     x[2].raw()
-    y[2].middle()
+    y[1].middle()
     x[1].middle()
     x[3].raw()
-    y[3].middle()
+    lay(0)
     x[2].middle()
-    settle(1, 0)
-    final[1].far()
-    settle(0, 2)
-    final[0].behind()
-    final[0].middle()
+    y[2].middle()
     x[3].middle()
-    settle(1, 1)
-    final[1].ahead()
-    settle(1, 2)
-    final[1].behind()
-    final[1].middle()
-    settle(0, 3)
-    settle(1, 3)
-    sent, passed = [], []
-    for h in range(2):
-        for q in range(2):
-            at = starts[h] + q * widths[h]
-            own = stream[span(seq.me, rows), pl.ds(pl.multiple_of(ten.me * cols + at, 128), widths[h])]
-            packed[span(seq.me, rows), at:at + widths[h]] = (
-                own.astype(f32) + final[h].total(q)
-            ).astype(bf16)
-        sent.append(both(packed.at[span(seq.me, rows), pl.ds(starts[h], 2 * widths[h])], seq))
-    for h in range(2):
-        sent[h][0].wait_recv()
-        passed.append(hop(packed.at[span(seq.at(3), rows), pl.ds(starts[h], widths[h])], seq.next))
-        sent[h][1].wait_recv()
-        passed.append(hop(packed.at[span(seq.at(1), rows), pl.ds(starts[h] + widths[h], widths[h])], seq.prev))
+    settle(0)
+    final.far()
+    e[0].middle()
+    lay(1)
+    settle(1)
+    final.ahead()
+    settle(2)
+    final.behind()
+    final.middle()
+    e[1].middle()
+    lay(2)
+    settle(3)
+    for q in range(2):
+        tail[half_of(seq.me, q), :] = final.total(q).astype(bf16)
+    mine = tail.at[span(seq.me, rows), :]
+    sent = both(mine, seq)
+    e[2].middle()
+    write(0)
+    sent[0].wait_recv()
+    passed = [hop(tail.at[half_of(seq.at(3), 0)], seq.next)]
+    sent[1].wait_recv()
+    passed.append(hop(tail.at[half_of(seq.at(1), 1)], seq.prev))
+    write(1)
     for copy in passed:
         copy.wait_recv()
-    query = lax.broadcasted_iota(jnp.int32, (out_ref.shape[0], 1), 0) + seq.me * out_ref.shape[0]
-    slot = lane_ref[0:1, 0:size]
-    for w, begin in enumerate(begins[1:], 1):
-        row = lax.broadcasted_iota(jnp.int32, slot.shape, 1) + begin
-        later = jnp.where(row >= w * size, lane_ref[0:1, begin:begin + size], -1)
-        slot = jnp.where(turn == w, later, slot)
-    spread = jnp.where(slot == query, 1.0, 0.0).astype(bf16)
-    out_ref[...] = (before_ref[...].astype(f32) + dot(spread, packed[...], PLAIN)).astype(bf16)
+    out_ref[:, cols - slim:] = (
+        base[:, cols - slim:] + dot(spread[span(seq.me, 2 * part_rows), :], tail[...], PLAIN)
+    ).astype(bf16)
+    write(2)
     c.drain()
 
 
@@ -576,8 +621,9 @@
     features = gain.shape[1]
     units = w_gate.shape[0]
     rows = size // RING
-    wide, slim = 3 * cols // 8, cols // 8
-    count = 6 + 40 + 60 + 8
+    slots = part.shape[0]
+    quarter, slim = cols // 4, 3 * cols // 8
+    count = 6 + 40 + 18 + 18 + 24 + 6 + 4
     vmem = pl.BlockSpec(memory_space=VMEM)
     hbm = pl.BlockSpec(memory_space=pltpu.HBM)
     dma = pltpu.SemaphoreType.DMA
@@ -593,19 +639,22 @@
             VMEM((size, features), bf16),
             VMEM((size, 128), f32),
             VMEM((size // 2, units), f32),
-            VMEM((size // 2, units), bf16),
+            VMEM((size, units), bf16),
             VMEM((2, size, 128), f32),
-            VMEM((size, cols), bf16),
+            VMEM((size, quarter), bf16),
             VMEM((units, features), bf16),
             VMEM((units, features), bf16),
             VMEM((units, features), bf16),
             VMEM((8, rows, cols // 2), bf16),
-            VMEM((RING, 8, rows, wide), bf16),
-            VMEM((RING, 8, rows, slim), bf16),
-            VMEM((RING, rows, 2 * wide), bf16),
-            VMEM((RING, rows, 2 * slim), bf16),
-            VMEM((8, rows, wide), bf16),
-            VMEM((8, rows, slim), bf16),
+            VMEM((3, 8, size // 2, quarter), bf16),
+            VMEM((3, 8, slots // RING // 2, quarter), bf16),
+            VMEM((RING, 8, rows // 2, slim), bf16),
+            VMEM((RING, rows, slim), bf16),
+            VMEM((8, rows // 2, slim), bf16),
+            VMEM((slots, size), bf16),
+            VMEM((3, slots, quarter), bf16),
+            VMEM((slots // RING, cols), f32),
+            VMEM((size, slim), bf16),
             dma((3,)), dma((count,)), dma((count,)),
         ],
         compiler_params=pltpu.CompilerParams(

time: 150 us -> 143 us (0.953)
  Pallas kernels: 145 us -> 139 us
    pallas_call x1, Pallas kernels: 99.9 us -> 93.9 us  [packed_layer(): pl.pallas_call(layer_kernel, out_shape=jax.ShapeDtypeStruct(before.shape,...]
where the time goes in v3:
time: 143 us; the launch traced here: 142 us
  Pallas kernels  139 us (97%)
  local copies, waits for them, and re-layouts  1.65 us (1%)
  loops' own time  1.44 us (1%)
    pallas_call x1, Pallas kernels, packed_layer(): pl.pallas_call(layer_kernel, out_shape=jax.ShapeDtypeStruct(before.shape,...  93.9 us
    pallas_call x1, Pallas kernels, attend(): pl.pallas_call(functools.partial(attention_kernel, replicas), out_shape=(...  45 us

profile of v3, /device:TPU:32, one launch (start us, length us, event | category | flops | bytes accessed | tf_op | source)
XLA Modules:
  0.0 142.0 jit_solution(9160409064616916677)
XLA Ops:
  0.0 0.0 copy-start
  0.0 0.0 copy-start.1
  0.0 45.0 %attend.1 = (bf16[1024,1024]{1,0:T(8,128)(2,1)S(1)}, bf16[1024,1024]{1,0:T(8,128)(2,1)}, f32[1024,128]{1,0:T(8,128)S(1)}, s32[8,1024]{1,0:T(8,128)S(1)}, s32[1]{0:T(128)}) custom-call(s32[1,4]{1,0:T(1,128)} %req_ref.1, s32[1,4]{1,0:T(1,128)} %len_ref.1, s32[2,1024]{1,0:T(2,128)} %bitcast.37, bf16[256,1024]{1,0:T(8,128)(2,1)} %bitcast.33, ...), custom_call_target="tpu_custom_call" | custom-call | tf_op jit(solution)/shard_map/attend/pallas_call | solution.py:304
  45.0 0.1 broadcast_in_dim.12
  45.1 0.0 copy-done
  45.1 0.0 copy-done.1
  45.1 96.1 %while.10 = (s32[]{:T(128)}, bf16[256,1024]{1,0:T(8,128)(2,1)S(1)}, s32[]{:T(128)}, f32[4096]{0:T(1024)S(1)}, bf16[4096,8]{0,1:T(8,128)(2,1)S(1)}, /*index=5*/bf...) while((s32[]{:T(128)}, bf16[256,1024]{1,0:T(8,128)(2,1)S(1)}, ...), condition=%wide.region_1.0_spmd, body=%wide.region_0.0_spmd.sunk | while | flops 2 | bytes 1048709 | solution.py:683
  45.9 0.8 copy.24.before_ref
  46.7 93.9 %layer.1 = bf16[256,1024]{1,0:T(8,128)(2,1)S(1)} custom-call(s32[1]{0:T(128)} %bitcast.21.turn_ref, bf16[1024,1024]{1,0:T(8,128)(2,1)S(1)} %get-tuple-element.211.part_ref, bf16[1024,1024]{1,0:T(8,128)(2,1)} %get-tuple-element.212.res_ref, f32[1024,128]{1,0:T(8,128)S(1)} %get-tuple-element.213.delta_ref, s32[8,1024]{1,0:T(8,128)S(1)} %get-tuple-element.214.lane_ref, ...), custom_call_target="tpu_custom_call" | custom-call | tf_op jit(solution)/shard_map/while/body/layer/pallas_call | solution.py:630
  141.2 0.8 copy.25
Async XLA Ops:
  0.0 45.1 %copy-start = (bf16[4096,8]{0,1:T(8,128)(2,1)S(1)}, bf16[4096,8]{0,1:T(8,128)(2,1)}, u32[]{:S(2)}) copy-start(bf16[4096,8]{0,1:T(8,128)(2,1)} %param.24) | copy-start | bytes 196612
  0.0 45.1 %copy-start.1 = (f32[4096]{0:T(1024)S(1)}, f32[4096]{0:T(1024)}, u32[]{:S(2)}) copy-start(f32[4096]{0:T(1024)} %param.23) | copy-start | bytes 49156
